TPU v7x, 8 devices: a whole 2x2x1 slice. The times are simulated.
8 devices in a mesh: tp: 2 (over z, y), ep: 4 (over x, core).
Axes of the slice: x: 2, y: 2, z: 1, core: 2. Of those that a mesh axis runs over, the one named last changes fastest.
Arguments:
- x_norm: bfloat16 [8192, 2304], P(('ep', 'tp'))
- route_idx: int32 [8192, 2], P(('ep', 'tp'))
- route_slot: int32 [8192, 2], P(('ep', 'tp'))
- w_router: bfloat16 [2304, 8], replicated
- b_router: float32 [8], replicated
- w_gate_up: bfloat16 [8, 2304, 11520], P('ep', None, 'tp')
- b_gate_up: float32 [8, 11520], P('ep', 'tp')
- w_down: bfloat16 [8, 5760, 2304], P('ep', 'tp')
- b_down: float32 [8, 2304], P('ep')
- d_out: bfloat16 [8192, 2304], P(('ep', 'tp'))
Outputs:
- output 1: bfloat16 [8192, 2304], P(('ep', 'tp'))
- output 2: bfloat16 [8192, 2304], P(('ep', 'tp'))
- output 3: bfloat16 [8, 2304, 11520], P('ep', None, 'tp')
- output 4: float32 [8, 11520], P('ep', 'tp')
- output 5: bfloat16 [8, 5760, 2304], P('ep', 'tp')
- output 6: float32 [8, 2304], P('ep')
- output 7: float32 [2304, 8], replicated
- output 8: float32 [8], replicated
All inputs are finite; a program needn't handle non-finite values.
Results may differ from a plain program's by a relative error of at most 0.0133159.
Values are sent between devices in bfloat16 or wider.
A program may use at most 1 GiB of HBM per device.

v0:
```python
import jax
import jax.numpy as jnp
from jax import lax
from jax.sharding import PartitionSpec as P

CLAMP_LIMIT = 7.0
SWIGLU_ALPHA = 1.702


def clamped_swiglu(h_pair):
    gate_val = jnp.minimum(h_pair[..., 0], CLAMP_LIMIT)
    up_val = jnp.clip(h_pair[..., 1], -CLAMP_LIMIT, CLAMP_LIMIT)
    return gate_val * jax.nn.sigmoid(SWIGLU_ALPHA * gate_val) * (up_val + 1.0)


def solution(mesh):
    tp_count = mesh.shape['tp']
    ep_count = mesh.shape['ep']
    tok_spec = P(('ep', 'tp'), None)

    def device_fn(x_loc, idx_loc, slot_loc, w_router, b_router, w_gate_up, b_gate_up, w_down, b_down, dy_loc):
        tok_count, model_dim = x_loc.shape
        top_k = idx_loc.shape[1]
        n_experts = w_router.shape[1]
        local_experts = w_gate_up.shape[0]
        shard_width = w_gate_up.shape[2] // 2
        capacity = 2 * tok_count * top_k // n_experts
        buf_rows = n_experts * capacity
        tp_index = lax.axis_index('tp')

        def dispatch(buf_in):
            gathered = lax.all_gather(buf_in.reshape(n_experts, capacity, model_dim), 'tp', axis=0)
            moved = lax.all_to_all(gathered, 'ep', 1, 1, tiled=True)
            return moved.reshape(tp_count, ep_count, local_experts, capacity, model_dim)

        def collect(part_in):
            back = lax.all_to_all(part_in.reshape(tp_count, n_experts, capacity, model_dim), 'ep', 1, 1, tiled=True)
            per_shard = lax.all_to_all(back, 'tp', 0, 0, tiled=True)
            return jnp.sum(per_shard, axis=0, dtype=jnp.float32).astype(jnp.bfloat16).reshape(buf_rows, model_dim)

        logits = jnp.dot(x_loc, w_router, preferred_element_type=jnp.float32) + b_router[None, :]
        expert_hot = idx_loc[:, :, None] == jnp.arange(n_experts)[None, None, :]
        picked = jnp.sum(jnp.where(expert_hot, logits[:, None, :], 0.0), axis=2)
        gate_w = jax.nn.softmax(picked, axis=1)
        flat_pos = jnp.where(slot_loc >= 0, idx_loc * capacity + slot_loc, -1)
        pick_mat = (flat_pos[:, :, None] == jnp.arange(buf_rows)[None, None, :]).astype(jnp.bfloat16)
        send_mat = jnp.max(pick_mat, axis=1)
        send_rows = jnp.einsum('tp,td->pd', send_mat, x_loc, preferred_element_type=jnp.float32).astype(jnp.bfloat16)

        recv_rows = dispatch(send_rows)
        hidden_pre = jnp.einsum('sgecd,edf->sgecf', recv_rows, w_gate_up, preferred_element_type=jnp.float32) + b_gate_up[None, None, :, None, :]
        h_pair = hidden_pre.reshape(hidden_pre.shape[:-1] + (shard_width, 2))
        act_f32, act_pull = jax.vjp(clamped_swiglu, h_pair)
        act_val = act_f32.astype(jnp.bfloat16)
        bias_on = (tp_index == 0).astype(jnp.float32)
        part_out = jnp.einsum('sgecf,efd->sgecd', act_val, w_down, preferred_element_type=jnp.float32)
        part_out = (part_out + bias_on * b_down[None, None, :, None, :]).astype(jnp.bfloat16)
        y_buf = collect(part_out)
        y_pick = jnp.einsum('tkp,pd->tkd', pick_mat, y_buf, preferred_element_type=jnp.float32)
        moe_out = jnp.sum(gate_w[:, :, None] * y_pick, axis=1).astype(jnp.bfloat16)

        d_out32 = dy_loc.astype(jnp.float32)
        d_gate = jnp.sum(y_pick * d_out32[:, None, :], axis=2)
        d_picked = gate_w * (d_gate - jnp.sum(gate_w * d_gate, axis=1, keepdims=True))
        d_logits = jnp.sum(jnp.where(expert_hot, d_picked[:, :, None], 0.0), axis=1)
        d_copy = (gate_w[:, :, None] * d_out32[:, None, :]).astype(jnp.bfloat16)
        d_send = jnp.einsum('tkp,tkd->pd', pick_mat, d_copy, preferred_element_type=jnp.float32).astype(jnp.bfloat16)
        d_recv = dispatch(d_send)
        grad_w_down = jnp.einsum('sgecf,sgecd->efd', act_val, d_recv, preferred_element_type=jnp.float32).astype(jnp.bfloat16)
        grad_b_down = jnp.sum(d_recv, axis=(0, 1, 3), dtype=jnp.float32)
        d_act = jnp.einsum('sgecd,efd->sgecf', d_recv, w_down, preferred_element_type=jnp.float32)
        d_pair = act_pull(d_act)[0]
        d_hidden = d_pair.reshape(hidden_pre.shape)
        grad_b_gate_up = jnp.sum(d_hidden, axis=(0, 1, 3))
        d_hidden_b = d_hidden.astype(jnp.bfloat16)
        grad_w_gate_up = jnp.einsum('sgecd,sgecf->edf', recv_rows, d_hidden_b, preferred_element_type=jnp.float32).astype(jnp.bfloat16)
        d_rows_part = jnp.einsum('sgecf,edf->sgecd', d_hidden_b, w_gate_up, preferred_element_type=jnp.float32).astype(jnp.bfloat16)
        d_rows = collect(d_rows_part)
        d_logits_b = d_logits.astype(jnp.bfloat16)
        d_x = jnp.einsum('tp,pd->td', send_mat, d_rows, preferred_element_type=jnp.float32) + jnp.einsum('te,de->td', d_logits_b, w_router, preferred_element_type=jnp.float32)
        grad_w_router = lax.psum(jnp.einsum('td,te->de', x_loc, d_logits_b, preferred_element_type=jnp.float32), ('tp', 'ep'))
        grad_b_router = lax.psum(jnp.sum(d_logits, axis=0), ('tp', 'ep'))
        return (moe_out, d_x.astype(jnp.bfloat16), grad_w_gate_up, grad_b_gate_up, grad_w_down, grad_b_down, grad_w_router, grad_b_router)

    in_specs = (tok_spec, tok_spec, tok_spec, P(None, None), P(None), P('ep', None, 'tp'), P('ep', 'tp'), P('ep', 'tp', None), P('ep', None), tok_spec)
    out_specs = (tok_spec, tok_spec, P('ep', None, 'tp'), P('ep', 'tp'), P('ep', 'tp', None), P('ep', None), P(None, None), P(None))
    return jax.shard_map(device_fn, mesh=mesh, in_specs=in_specs, out_specs=out_specs, check_vma=False)
```

profile of v0, /device:TPU:0, one launch (start us, length us, event | category | flops | bytes accessed | tf_op | source)
XLA Modules:
  0.0 4082.8 jit_solution(17052855416652986781)
XLA Ops:
  7.2 0.0 copy-start
  7.2 0.0 all-gather.3.cloned.1.call-start
  7.2 0.7 compare_select_fusion
  8.0 0.0 copy-start.6
  8.0 12.6 fusion.42
  20.6 26.8 convolution_convert_fusion
  47.4 0.0 all-gather.3.cloned.1.call-update
  47.4 0.2 all-gather.5.cloned.1.call-start
  47.6 6.6 convert_element_type.69
  54.3 3.6 convolution_add_fusion
  58.1 0.6 copy-done.10
  58.7 0.0 copy-start.14
  58.7 10.7 iota_compare_fusion.9
  69.3 47.1 %bitcast_convert_fusion.2 = bf16[4096,2304]{1,0:T(8,128)(2,1)} fusion(f32[1024,2304]{1,0:T(8,128)} %convert_element_type.69, f32[1024,2]{0,1:T(2,128)S(1)} %fusion.50, pred[1024,2,4096]{0,2,1:T(32,128)(4,1)} %iota_compare_fusion.9), kind=kOutput, calls=%fused_computation.43 | convolution fusion | flops 38673580032 | bytes 36708352 | tf_op jit(solution)/shard_map/tkp,tkd->pd/dot_general | solution.py:67
  116.5 0.0 all-gather.5.cloned.1.call-update
  116.5 367.7 %all-gather.3.cloned.1.call-done = bf16[2,8,512,2304]{3,2,1,0:T(8,128)(2,1)} async-done(((bf16[1,8,512,2304]{3,2,1,0:T(8,128)(2,1)}), bf16[2,8,512,2304]{3,2,1,0:T(8,128)(2,1)}) %all-gather.3.cloned.1.call-update) | async-done | bytes 37748752 | tf_op jit(solution)/shard_map/all_gather | solution.py:32
  484.2 25.4 copy.118
  509.6 10.6 all-to-all-start
  520.3 0.6 broadcast_multiply_fusion
  520.9 399.2 %all-gather.5.cloned.1.call-done = bf16[2,8,512,2304]{3,2,1,0:T(8,128)(2,1)} async-done(((bf16[1,8,512,2304]{3,2,1,0:T(8,128)(2,1)}), bf16[2,8,512,2304]{3,2,1,0:T(8,128)(2,1)}) %all-gather.5.cloned.1.call-update) | async-done | bytes 37748752 | tf_op jit(solution)/shard_map/all_gather | solution.py:32
  920.1 25.4 copy.128
  945.5 11.1 all-to-all-start.3
  956.6 247.2 %add_bitcast_fusion = f32[2,4,2,512,5760]{4,3,1,0,2:T(8,128)} fusion(f32[2,5760]{1,0:T(2,128)S(1)} %copy-done.17, bf16[2,2304,5760]{2,1,0:T(8,128)(2,1)} %param.15, bf16[2,4,2,512,2304]{4,3,0,2,1:T(8,128)(2,1)} %bitcast.2), kind=kOutput, calls=%fused_computation.1 | convolution fusion | flops 217479905280 | bytes 279622656 | tf_op jit(solution)/shard_map/sgecd,edf->sgecf/dot_general | solution.py:51
  1203.8 271.5 %copy.121 = f32[2,4,2,512,5760]{3,2,4,1,0:T(2,128)} copy(f32[2,4,2,512,5760]{4,3,1,0,2:T(8,128)} %add_bitcast_fusion) | data formatting | bytes 377487360 | tf_op jit(solution)/shard_map/add | solution.py:51
  1475.4 125.7 %fusion.52 = (f32[2,4,2,512,2880,1]{3,2,5,4,1,0:T(2,128)}, f32[2,4,2,512,2880,1]{3,2,5,4,1,0:T(2,128)}) fusion(f32[2,4,2,512,2880,2]{3,2,5,4,1,0:T(2,128)} %bitcast.6), kind=kLoop, calls=%fused_computation.78 | loop fusion | bytes 377487360 | tf_op jit(solution)/shard_map/jvp()/slice | solution.py:11
  1601.1 120.6 %fusion.26 = f32[2,2,4,512,2880]{3,4,2,1,0:T(8,128)} fusion(bf16[2,4,2,512,2304]{4,3,0,2,1:T(8,128)(2,1)} %bitcast.18, bf16[2,2880,2304]{2,1,0:T(8,128)(2,1)} %param.17), kind=kOutput, calls=%fused_computation.41 | convolution fusion | flops 108716359680 | bytes 158662656 | tf_op jit(solution)/shard_map/sgecd,efd->sgecf/dot_general | solution.py:71
  1721.6 195.8 %fusion.7 = (f32[2,4,2,512,2880,1]{3,4,1,0,2,5:T(8,128)}, f32[2,4,2,512,2880,1]{3,4,1,0,2,5:T(8,128)}, bf16[2,4,2,512,2880]{3,4,1,0,2:T(8,128)(2,1)}) fusion(f32[2,2,4,512,2880]{3,4,2,1,0:T(8,128)} %fusion.26, f32[2,4,2,512,2880,1]{3,2,5,4,1,0:T(2,128)} %get-tuple-element.18, f32[2,4,2,512,2880,1]{3,2,5,4,1,0:T(2,128)} %get-tuple-element.17), kind=kLoop, calls=%fused_computation.12 | loop fusion | flops 825753600 | bytes 519045120 | tf_op jit(solution)/shard_map/transpose(jvp())/broadcast_in_dim | solution.py:12
  1917.5 129.5 %fusion.23 = bf16[2,4,2,512,2304]{4,3,1,0,2:T(8,128)(2,1)} fusion(f32[2,2304]{1,0:T(2,128)S(1)} %copy-done.13, bf16[2,4,2,512,2880]{3,4,1,0,2:T(8,128)(2,1)} %get-tuple-element.16, bf16[2,2880,2304]{2,1,0:T(8,128)(2,1)} %param.17), kind=kOutput, calls=%fused_computation.38 | convolution fusion | flops 108754108416 | bytes 111495168 | tf_op jit(solution)/shard_map/sgecf,efd->sgecd/dot_general | solution.py:56
  2046.9 25.5 copy.124
  2072.4 25.4 copy.125
  2097.8 10.7 all-to-all-start.1
  2108.5 90.2 %fusion = (f32[2,2880,2]{1,0,2:T(2,128)}, bf16[2,4,2,512,2880,2]{3,4,1,0,2,5:T(8,128)(2,1)}) fusion(f32[2,4,2,512,2880,1]{3,4,1,0,2,5:T(8,128)} %get-tuple-element.13, f32[2,4,2,512,2880,1]{3,4,1,0,2,5:T(8,128)} %get-tuple-element.12), kind=kLoop, calls=%fused_computation.2 | loop fusion | flops 141546240 | bytes 283161600 | tf_op jit(solution)/shard_map/reduce_sum | solution.py:74
  2198.7 168.0 %copy.131 = bf16[2,4,2,512,2880,2]{3,2,5,4,1,0:T(2,128)(2,1)} copy(bf16[2,4,2,512,2880,2]{3,4,1,0,2,5:T(8,128)(2,1)} %get-tuple-element.15) | data formatting | bytes 188743680 | tf_op jit(solution)/shard_map/convert_element_type | solution.py:75
  2366.6 322.2 %convert_bitcast_fusion = bf16[2,4,2,512,2304]{4,3,1,0,2:T(8,128)(2,1)} fusion(bf16[2,2304,5760]{2,1,0:T(8,128)(2,1)} %param.15, bf16[2,4,2,512,5760]{3,2,4,1,0:T(2,128)(2,1)} %bitcast.26), kind=kOutput, calls=%fused_computation.45 | convolution fusion | flops 217451593728 | bytes 185204736 | tf_op jit(solution)/shard_map/sgecf,edf->sgecd/dot_general | solution.py:77
  2688.8 25.5 copy.133
  2714.3 25.5 copy.134
  2739.9 10.5 all-to-all-start.4
  2750.4 25.5 copy.126
  2775.8 381.9 %all-to-all-done.4 = bf16[2,8,512,2304]{3,2,0,1:T(8,128)(2,1)} async-done(((bf16[2,8,512,2304]{3,2,0,1:T(8,128)(2,1)}), bf16[2,8,512,2304]{3,2,0,1:T(8,128)(2,1)}, u32[]{:S(2)}, u32[]{:S(2)}) %all-to-all-start.4) | async-done | bytes 37748768 | tf_op jit(solution)/shard_map/all_to_all | solution.py:37
  3157.8 14.5 all-to-all-start.2
  3172.3 306.6 %bitcast_convert_fusion = bf16[2,2304,5760]{2,1,0:T(8,128)(2,1)} fusion(bf16[2,4,2,512,5760]{3,2,4,1,0:T(2,128)(2,1)} %bitcast.26, bf16[2,4,2,512,2304]{4,3,0,2,1:T(8,128)(2,1)} %bitcast.2), kind=kOutput, calls=%fused_computation.5 | convolution fusion | flops 217459261440 | bytes 185204736 | tf_op jit(solution)/shard_map/sgecd,sgecf->edf/dot_general | solution.py:76
  3478.9 25.5 copy.135
  3504.4 74.6 %all-to-all-done.2 = bf16[2,8,512,2304]{3,2,1,0:T(8,128)(2,1)} async-done(((bf16[2,8,512,2304]{3,2,1,0:T(8,128)(2,1)}), bf16[2,8,512,2304]{3,2,1,0:T(8,128)(2,1)}, u32[]{:S(2)}, u32[]{:S(2)}) %all-to-all-start.2) | async-done | bytes 37748768 | tf_op jit(solution)/shard_map/all_to_all | solution.py:38
  3579.0 14.5 all-to-all-start.5
  3593.5 0.0 all-reduce.4.cloned.1.call-start
  3593.5 0.0 copy-start.3
  3593.5 131.4 %bitcast_convert_fusion.1 = bf16[2,2880,2304]{2,1,0:T(8,128)(2,1)} fusion(bf16[2,4,2,512,2304]{4,3,0,2,1:T(8,128)(2,1)} %bitcast.18, bf16[2,4,2,512,2880]{3,4,1,0,2:T(8,128)(2,1)} %get-tuple-element.16), kind=kOutput, calls=%fused_computation.33 | convolution fusion | flops 108729630720 | bytes 111476736 | tf_op jit(solution)/shard_map/sgecf,sgecd->efd/dot_general | solution.py:69
  3724.9 0.9 copy.138
  3725.8 2.7 reduce_sum.123
  3728.4 12.8 convert_reduce_fusion
  3741.3 0.0 copy-start.7
  3741.3 0.6 reduce_sum.126
  3742.0 23.5 reduce_sum.116
  3765.5 0.0 slice-start.1
  3765.5 53.2 %multiply_reduce_fusion = (f32[1024,2]{0,1:T(2,128)S(1)}, bf16[1024,2304]{1,0:T(8,128)(2,1)}) fusion(f32[1024,2304]{1,0:T(8,128)} %convert_element_type.69, f32[1024,2]{0,1:T(2,128)S(1)} %copy-done.15, bf16[4096,2304,1]{1,0,2:T(8,128)(2,1)} %bitcast.121, s32[1024,2]{0,1:T(2,128)S(1)} %copy-done.7), kind=kOutput, calls=%fused_computation.53 | convolution fusion | flops 38679609344 | bytes 33054720 | tf_op jit(solution)/shard_map/tkp,pd->tkd/dot_general | solution.py:59
  3818.8 0.1 select_reduce_fusion
  3819.0 1.4 convolution_bitcast_fusion
  3820.3 0.0 all-reduce.4.cloned.1.call-update
  3820.3 5.1 fusion.53
  3825.4 175.2 %all-to-all-done.5 = bf16[2,8,512,2304]{3,2,1,0:T(8,128)(2,1)} async-done(((bf16[2,8,512,2304]{3,2,1,0:T(8,128)(2,1)}), bf16[2,8,512,2304]{3,2,1,0:T(8,128)(2,1)}, u32[]{:S(2)}, u32[]{:S(2)}) %all-to-all-start.5) | async-done | bytes 37748768 | tf_op jit(solution)/shard_map/all_to_all | solution.py:38
  4000.6 23.4 reduce_sum.118
  4024.1 28.3 add_convert_fusion.1
  4052.4 22.2 psum.15
  4074.5 1.5 copy.197
  (45 shorter events, 0.3 us)
Async XLA Ops:
  7.2 47.1 %copy-start = (bf16[2304,8]{0,1:T(8,128)(2,1)S(1)}, bf16[2304,8]{0,1:T(8,128)(2,1)}, u32[]{:S(2)}) copy-start(bf16[2304,8]{0,1:T(8,128)(2,1)} %param.13) | copy-start | bytes 110596
  7.2 477.0 %all-gather.3.cloned.1.call-start = ((), (), s32[]{:S(2)}) async-start(), calls=%async_computation.6 | async-start | bytes 56623104 | tf_op jit(solution)/shard_map/all_gather | solution.py:32
  8.0 50.7 %copy-start.6 = (s32[1024,2]{0,1:T(2,128)}, s32[1024,2]{0,1:T(2,128)S(1)}, u32[]{:S(2)}) copy-start(s32[1024,2]{0,1:T(2,128)S(1)} %compare_select_fusion) | copy-start | bytes 24580
  20.6 33.7 copy-start.16
  47.4 10.5 copy-start.8
  47.4 872.7 %all-gather.5.cloned.1.call-start = ((), (), s32[]{:S(2)}) async-start(), calls=%async_computation.7 | async-start | bytes 56623104 | tf_op jit(solution)/shard_map/all_gather | solution.py:32
  58.0 58.5 %copy-start.1 = (f32[1024,2]{0,1:T(2,128)}, f32[1024,2]{0,1:T(2,128)S(1)}, u32[]{:S(2)}) copy-start(f32[1024,2]{0,1:T(2,128)S(1)} %select_reduce_fusion.2) | copy-start | bytes 24580
  58.0 58.4 %copy-start.4 = (f32[1024]{0:T(1024)}, f32[1024]{0:T(1024)S(1)}, u32[]{:S(2)}) copy-start(f32[1024]{0:T(1024)S(1)} %reduce_max.18) | copy-start | bytes 12292
  58.0 0.6 copy-start.10
  58.7 57.8 %copy-start.14 = (f32[1024,2]{0,1:T(2,128)}, f32[1024,2]{0,1:T(2,128)S(1)}, u32[]{:S(2)}) copy-start(f32[1024,2]{0,1:T(2,128)S(1)} %fusion.50) | copy-start | bytes 24580
  509.6 10.7 copy-start.12
  509.6 435.9 %all-to-all-start = ((bf16[2,8,512,2304]{3,2,0,1:T(8,128)(2,1)}), bf16[2,8,512,2304]{3,2,0,1:T(8,128)(2,1)}, u32[]{:S(2)}, u32[]{:S(2)}) async-start(bf16[2,8,512,2304]{3,2,0,1:T(8,128)(2,1)} %copy.118), calls=%async_computation | async-start | bytes 75497472 | tf_op jit(solution)/shard_map/all_to_all | solution.py:33
  945.5 11.1 copy-start.17
  945.5 655.6 %all-to-all-start.3 = ((bf16[2,8,512,2304]{3,2,0,1:T(8,128)(2,1)}), bf16[2,8,512,2304]{3,2,0,1:T(8,128)(2,1)}, u32[]{:S(2)}, u32[]{:S(2)}) async-start(bf16[2,8,512,2304]{3,2,0,1:T(8,128)(2,1)} %copy.128), calls=%async_computation.3 | async-start | bytes 75497472 | tf_op jit(solution)/shard_map/all_to_all | solution.py:33
  1721.6 195.8 %copy-start.13 = (f32[2,2304]{1,0:T(2,128)S(1)}, f32[2,2304]{1,0:T(2,128)}, u32[]{:S(2)}) copy-start(f32[2,2304]{1,0:T(2,128)} %broadcast_multiply_fusion) | copy-start | bytes 55300
  2097.8 642.1 %all-to-all-start.1 = ((bf16[2,8,512,2304]{3,2,0,1:T(8,128)(2,1)}), bf16[2,8,512,2304]{3,2,0,1:T(8,128)(2,1)}, u32[]{:S(2)}, u32[]{:S(2)}) async-start(bf16[2,8,512,2304]{3,2,0,1:T(8,128)(2,1)} %copy.125), calls=%async_computation.1 | async-start | bytes 75497472 | tf_op jit(solution)/shard_map/all_to_all | solution.py:37
  2739.9 417.9 %all-to-all-start.4 = ((bf16[2,8,512,2304]{3,2,0,1:T(8,128)(2,1)}), bf16[2,8,512,2304]{3,2,0,1:T(8,128)(2,1)}, u32[]{:S(2)}, u32[]{:S(2)}) async-start(bf16[2,8,512,2304]{3,2,0,1:T(8,128)(2,1)} %copy.134), calls=%async_computation.4 | async-start | bytes 75497472 | tf_op jit(solution)/shard_map/all_to_all | solution.py:37
  3157.8 421.2 %all-to-all-start.2 = ((bf16[2,8,512,2304]{3,2,1,0:T(8,128)(2,1)}), bf16[2,8,512,2304]{3,2,1,0:T(8,128)(2,1)}, u32[]{:S(2)}, u32[]{:S(2)}) async-start(bf16[2,8,512,2304]{3,2,1,0:T(8,128)(2,1)} %copy.126), calls=%async_computation.2 | async-start | bytes 75497472 | tf_op jit(solution)/shard_map/all_to_all | solution.py:38
  3579.0 421.6 %all-to-all-start.5 = ((bf16[2,8,512,2304]{3,2,1,0:T(8,128)(2,1)}), bf16[2,8,512,2304]{3,2,1,0:T(8,128)(2,1)}, u32[]{:S(2)}, u32[]{:S(2)}) async-start(bf16[2,8,512,2304]{3,2,1,0:T(8,128)(2,1)} %copy.135), calls=%async_computation.5 | async-start | bytes 75497472 | tf_op jit(solution)/shard_map/all_to_all | solution.py:38
  3593.5 481.1 %all-reduce.4.cloned.1.call-start = ((), (), s32[]{:S(2)}) async-start(), calls=%async_computation.8 | async-start | bytes 147456 | tf_op jit(solution)/shard_map/psum | solution.py:81
  3593.5 131.4 %copy-start.3 = (f32[2,2880,2]{1,0,2:T(2,128)S(1)}, f32[2,2880,2]{1,0,2:T(2,128)}, u32[]{:S(2)}) copy-start(f32[2,2880,2]{1,0,2:T(2,128)} %get-tuple-element.14) | copy-start | bytes 138244
  3741.3 24.2 copy-start.7
  3741.3 24.2 copy-start.15
  3742.0 76.9 %slice-start = ((s8[4718592]{0:T(1024)(128)(4,1)}), s8[524288]{0:T(1024)(128)(4,1)S(1)}, s32[]{:S(2)}) async-start(s8[4718592]{0:T(1024)(128)(4,1)} %bitcast.117), calls=%async_computation.9 | async-start | bytes 1048576
  3765.5 53.2 %copy-start.2 = (f32[1024,2]{0,1:T(2,128)S(1)}, f32[1024,2]{0,1:T(2,128)}, u32[]{:S(2)}) copy-start(f32[1024,2]{0,1:T(2,128)} %copy-done.1) | copy-start | bytes 24580
  3765.5 53.2 %copy-start.5 = (f32[1024]{0:T(1024)S(1)}, f32[1024]{0:T(1024)}, u32[]{:S(2)}) copy-start(f32[1024]{0:T(1024)} %copy-done.4) | copy-start | bytes 12292
  3765.5 53.2 %copy-start.11 = (f32[1024]{0:T(1024)S(1)}, f32[1024]{0:T(1024)}, u32[]{:S(2)}) copy-start(f32[1024]{0:T(1024)} %copy-done.10) | copy-start | bytes 12292
  3765.5 53.3 %copy-start.9 = (s32[1024,2]{0,1:T(2,128)S(1)}, s32[1024,2]{0,1:T(2,128)}, u32[]{:S(2)}) copy-start(s32[1024,2]{0,1:T(2,128)} %param.11) | copy-start | bytes 24580
  3765.5 53.4 %slice-start.1 = ((s8[4718592]{0:T(1024)(128)(4,1)}), s8[4194304]{0:T(1024)(128)(4,1)S(1)}, s32[]{:S(2)}) async-start(s8[4718592]{0:T(1024)(128)(4,1)} %bitcast.117), calls=%async_computation.10 | async-start | bytes 8388608
Sparse Core Ops, SparseCore 0:
  47.5 436.6 all-gather.2
  486.3 433.7 all-gather.4
  3820.5 42.9 all-reduce.3
where the time goes:
time: 4100 us; the launch traced here: 4080 us
  matrix products  1420 us (35%)
  waiting for transfers between devices  1400 us (34%)
  local copies, waits for them, and re-layouts  775 us (19%)
  other arithmetic  378 us (9%)
  starting transfers between devices  72.1 us (2%)
    all_gather x2, waiting for transfers between devices, dispatch(): lax.all_gather(buf_in.reshape(n_experts, capacity, model_dim), 'tp', axis=0)  767 us
    all_to_all x2, waiting for transfers between devices, collect(): lax.all_to_all(part_in.reshape(tp_count, n_experts, capacity, model_dim),...  382 us
    dot_general x1, matrix products, device_fn(): jnp.einsum('sgecf,edf->sgecd', d_hidden_b, w_gate_up, preferred_element_t...  322 us
    dot_general x1, matrix products, device_fn(): jnp.einsum('sgecd,sgecf->edf', recv_rows, d_hidden_b, preferred_element_t...  307 us
    add x1, local copies, waits for them, and re-layouts, device_fn(): jnp.einsum('sgecd,edf->sgecf', recv_rows, w_gate_up, preferred_element_ty...  272 us
    all_to_all x2, waiting for transfers between devices, collect(): per_shard = lax.all_to_all(back, 'tp', 0, 0, tiled=True)  250 us
    dot_general x1, matrix products, device_fn(): jnp.einsum('sgecd,edf->sgecf', recv_rows, w_gate_up, preferred_element_ty...  247 us
    broadcast_in_dim x1, other arithmetic, clamped_swiglu(): up_val = jnp.clip(h_pair[..., 1], -CLAMP_LIMIT, CLAMP_LIMIT)  196 us
  transfers between devices with their start and end apart: 9, of which 5 were waited for; matrix products, arithmetic and copies ran while one was open for 50% of the time, Pallas kernels for 0%

commit v1 on v0

v1 whole, which is shorter than its diff:
```python
import functools
import jax
import jax.numpy as jnp
from jax import lax
from jax.experimental import pallas as pl
from jax.experimental.pallas import tpu as pltpu
from jax.sharding import Mesh, PartitionSpec as P

ZERO = 0
ONE = 1
LANES = 128
LIMIT = 7.0
ALPHA = 1.702
WIN = 256
BLK = 256
FT = 512
GR = 16
F32 = jnp.float32
BF16 = jnp.bfloat16
I32 = jnp.int32
VMEM_MAX = 62 * 1024 * 1024
MT = 3


def params(n_axes, vmem=VMEM_MAX):
    return pltpu.CompilerParams(dimension_semantics=('arbitrary',) * n_axes, vmem_limit_bytes=vmem)


def dot(lhs, rhs):
    return lax.dot_general(lhs, rhs, (((ONE,), (ZERO,)), ((), ())), preferred_element_type=F32)


def dot_nt(lhs, rhs):
    return lax.dot_general(lhs, rhs, (((ONE,), (ONE,)), ((), ())), preferred_element_type=F32)


def dot_tn(lhs, rhs):
    return lax.dot_general(lhs, rhs, (((ZERO,), (ZERO,)), ((), ())), preferred_element_type=F32)


def mult(value, base):
    return pl.multiple_of(value, base)


class Table:
    def __init__(self, nw):
        self.nw = nw
        self.first, self.count, self.full, self.flat, self.part = (i * 4 * nw for i in range(5))
        base = 20 * nw
        self.end, self.cover, self.mid, self.list0, self.list1 = (base + 4 * i for i in range(5))
        self.seg = base + 20
        self.x = base + 21


def make_table(idx_t, slot_t, x_pos, c_pos, tp_pos, tab):
    tok = idx_t.shape[ONE]
    nw = tab.nw
    nb = tok // LANES
    col = idx_t // 4
    within = idx_t % 4
    local = jnp.where(within // 2 == c_pos, ZERO, 2) + within % 2
    expert = jnp.where((slot_t >= ZERO) & (col == x_pos), local, -ONE)
    ids = jnp.arange(4, dtype=I32)
    hot = jnp.any(expert[:, None, :] == ids[None, :, None], axis=ZERO)
    blocks = hot.astype(BF16).reshape(4, nb, LANES)
    tri = (jnp.arange(LANES)[:, None] <= jnp.arange(LANES)[None, :]).astype(BF16)
    incl = jnp.einsum('ebt,ts->ebs', blocks, tri, preferred_element_type=F32)
    sums = incl[:, :, 127]
    bid = jnp.arange(nb)
    same = (bid[:, None] // (nb // 2)) == (bid[None, :] // (nb // 2))
    before = (same & (bid[:, None] < bid[None, :])).astype(BF16)
    prefix = jnp.einsum('eb,bc->ec', sums.astype(BF16), before, preferred_element_type=F32)
    sums_i = sums.astype(I32)
    prefix_i = prefix.astype(I32)
    n_seg = jnp.sum(sums_i.reshape(4, 2, nb // 2), axis=2)
    pad_seg = (n_seg + GR - ONE) // GR * GR
    mid = pad_seg[:, ZERO]
    base_blk = jnp.where(bid[None, :] >= nb // 2, mid[:, None], ZERO)
    start = base_blk + prefix_i
    wpb = WIN // LANES
    w_start = start.reshape(4, nw, wpb)[:, :, ZERO]
    w_end = w_start + jnp.sum(sums_i.reshape(4, nw, wpb), axis=2)
    first = w_start // GR * GR
    count = ((w_end + GR - ONE) // GR * GR - first) // GR
    wid = jnp.arange(nw)
    last = (wid % (nw // 2)) == nw // 2 - ONE
    full = jnp.where(last[None, :], count, (w_end // GR * GR - first) // GR)
    flat = (jnp.cumsum(count, axis=ZERO) - count) * GR
    part = (w_start % GR != ZERO).astype(I32)
    end = mid + n_seg[:, ONE]
    cover = jnp.maximum((end + 127) // LANES * LANES, LANES)
    lists = (jnp.cumsum(pad_seg, axis=ZERO) - pad_seg)
    totals = jnp.sum(pad_seg, axis=ZERO)
    row = (start[:, :, None] + incl.astype(I32) - ONE).reshape(4, nw, WIN)
    flat_row = (row - first[:, :, None] + flat[:, :, None]).reshape(4, tok)
    pos = jnp.max(jnp.where(expert[:, None, :] == ids[None, :, None], flat_row[None], -ONE), axis=ONE)
    vec = jnp.concatenate([
        first.reshape(-ONE), count.reshape(-ONE), full.reshape(-ONE), flat.reshape(-ONE), part.reshape(-ONE),
        end, cover, mid, lists[:, ZERO], lists[:, ONE], jnp.stack([tp_pos, x_pos]).astype(I32)])
    return vec.astype(I32), pos.astype(I32), totals


def pair_matrix():
    i = lax.broadcasted_iota(I32, (256, 256), ZERO)
    n = lax.broadcasted_iota(I32, (256, 256), ONE)
    src = jnp.where(n < LANES, 2 * n, 2 * n - 255)
    return jnp.where(i == src, 1.0, 0.0).astype(BF16)


def pair_matrix_t():
    i = lax.broadcasted_iota(I32, (256, 256), ONE)
    n = lax.broadcasted_iota(I32, (256, 256), ZERO)
    src = jnp.where(n < LANES, 2 * n, 2 * n - 255)
    return jnp.where(i == src, 1.0, 0.0).astype(BF16)


def split_weights(w_gu):
    n_e, dim, width = w_gu.shape
    nf = pl.cdiv(width, 2 * FT)
    rows = dim // MT

    def body(w_ref, o_ref):
        f = pl.program_id(ONE)
        mat = pair_matrix()

        def go(valid):
            for g in range(2 * FT // 256):
                lo, hi = 256 * g, min(256 * g + 256, valid)
                if hi > lo:
                    res = dot(w_ref[ZERO, :, lo:hi], mat[:hi - lo]).astype(BF16)
                else:
                    res = jnp.zeros((rows, 256), BF16)
                o_ref[ZERO, ZERO, :, LANES * g:LANES * g + LANES] = res[:, :LANES]
                o_ref[ZERO, ZERO, :, FT + LANES * g:FT + LANES * g + LANES] = res[:, LANES:]

        @pl.when(f < nf - ONE)
        def _():
            go(2 * FT)

        @pl.when(f == nf - ONE)
        def _():
            go(width - (nf - ONE) * 2 * FT)

    return pl.pallas_call(
        body, name='split_weights', grid=(n_e, nf, MT),
        in_specs=[pl.BlockSpec((ONE, rows, 2 * FT), lambda e, f, r: (e, r, f))],
        out_specs=pl.BlockSpec((ONE, ONE, rows, 2 * FT), lambda e, f, r: (e, f, r, ZERO)),
        out_shape=jax.ShapeDtypeStruct((n_e, nf, dim, 2 * FT), BF16),
        compiler_params=params(3),
        cost_estimate=pl.CostEstimate(flops=2 * n_e * dim * width * 256, bytes_accessed=4 * n_e * dim * width, transcendentals=ZERO),
    )(w_gu)


def flat_blocks(tab_ref, tab, w):
    rows = tab_ref[tab.flat + 3 * tab.nw + w] + GR * tab_ref[tab.count + 3 * tab.nw + w]
    return (rows + BLK - ONE) // BLK


FLAT = 3 * BLK


def gather_rows(vec, pos, tokens, cap, tab, wk=None):
    tok, dim = tokens.shape
    nw = tab.nw

    def body(tab_ref, *refs):
        if wk is None:
            pos_ref, x_ref, out_ref, fb, carry, zero, sem, zsem = refs
        else:
            pos_ref, wk_ref, x_ref, out_ref, fb, carry, zero, sem, zsem = refs
        w = pl.program_id(ZERO)
        slot = lax.rem(w, 2)

        def drain(win, which):
            n = sum(tab_ref[tab.full + e * nw + win] for e in range(4))

            def one(_, c):
                pltpu.make_async_copy(fb.at[ZERO, pl.ds(ZERO, GR)], out_ref.at[ZERO, pl.ds(ZERO, GR)], sem.at[which]).wait()
                return c

            lax.fori_loop(ZERO, n, one, ZERO)

        @pl.when(w == ZERO)
        def _():
            zero[...] = jnp.zeros_like(zero)

        @pl.when(w >= 2)
        def _():
            drain(w - 2, slot)

        def block(b, c):
            j = lax.broadcasted_iota(I32, (BLK, WIN), ZERO) + b * BLK
            m0 = pos_ref[ZERO:ONE, :] == j
            m1 = pos_ref[ONE:2, :] == j
            hot = jnp.where(m0 | m1, 1.0, 0.0).astype(BF16)
            res = dot(hot, x_ref[...])
            if wk is not None:
                scale = jnp.where(m0, wk_ref[ZERO:ONE, :], 0.0) + jnp.where(m1, wk_ref[ONE:2, :], 0.0)
                res = res * jnp.sum(scale, axis=ONE, keepdims=True)
            fb[slot, pl.ds(mult(b * BLK, BLK), BLK), :] = res.astype(BF16)
            return c

        lax.fori_loop(ZERO, flat_blocks(tab_ref, tab, w), block, ZERO)

        for e in range(4):
            at = e * nw + w
            n_groups = tab_ref[tab.count + at]
            off = tab_ref[tab.flat + at]
            first = tab_ref[tab.first + at]

            @pl.when(n_groups > ZERO)
            def _():
                head = pl.ds(mult(off, GR), GR)

                @pl.when(tab_ref[tab.part + at] == ONE)
                def _():
                    fb[slot, head, :] = fb[slot, head, :] + carry[e]

                carry[e] = fb[slot, pl.ds(mult(off + GR * (n_groups - ONE), GR), GR), :]

            def send(g, c):
                pltpu.make_async_copy(
                    fb.at[slot, pl.ds(mult(off + GR * g, GR), GR)],
                    out_ref.at[e, pl.ds(mult(first + GR * g, GR), GR)], sem.at[slot]).start()
                return c

            lax.fori_loop(ZERO, tab_ref[tab.full + at], send, ZERO)

        @pl.when(w == nw - ONE)
        def _():
            for e in range(4):
                lo = (tab_ref[tab.end + e] + GR - ONE) // GR
                hi = tab_ref[tab.cover + e] // GR

                def fill(g, c):
                    pltpu.make_async_copy(zero, out_ref.at[e, pl.ds(mult(g * GR, GR), GR)], zsem).start()
                    return c

                lax.fori_loop(lo, hi, fill, ZERO)

                def done(g, c):
                    pltpu.make_async_copy(zero, out_ref.at[e, pl.ds(ZERO, GR)], zsem).wait()
                    return c

                lax.fori_loop(lo, hi, done, ZERO)
            drain(w - ONE, ONE - slot)
            drain(w, slot)

    args = [vec, pos] + ([] if wk is None else [wk]) + [tokens]
    small = pl.BlockSpec((2, WIN), lambda w, t: (ZERO, w))
    return pl.pallas_call(
        body, name='gather_rows',
        grid_spec=pltpu.PrefetchScalarGridSpec(
            num_scalar_prefetch=ONE, grid=(nw,),
            in_specs=[small] * (len(args) - 2) + [pl.BlockSpec((WIN, dim), lambda w, t: (w, ZERO))],
            out_specs=pl.BlockSpec(memory_space=pl.ANY),
            scratch_shapes=[pltpu.VMEM((2, FLAT, dim), BF16), pltpu.VMEM((4, GR, dim), BF16), pltpu.VMEM((GR, dim), BF16),
                            pltpu.SemaphoreType.DMA((2,)), pltpu.SemaphoreType.DMA]),
        out_shape=jax.ShapeDtypeStruct((4, cap, dim), BF16),
        compiler_params=params(ONE),
        cost_estimate=pl.CostEstimate(flops=8 * tok * 256 * dim, bytes_accessed=4 * tok * dim, transcendentals=ZERO),
    )(*args)


def swiglu_parts(h):
    gate, up = h[:, :FT], h[:, FT:]
    g = jnp.minimum(gate, LIMIT)
    u1 = jnp.clip(up, -LIMIT, LIMIT) + 1.0
    s = jax.nn.sigmoid(ALPHA * g)
    return gate, up, g, u1, s


def row_blocks(tab_ref, tab, expert, block):
    cover = tab_ref[tab.cover + expert]
    n_full = cover // BLK

    def whole(i, c):
        block(i, BLK)
        return c

    lax.fori_loop(ZERO, n_full, whole, ZERO)

    @pl.when(cover % BLK != ZERO)
    def _():
        block(n_full, LANES)


def expert_forward(vec, x_rows, wg, wd, bg, bd, half, lists, main_rows, tab):
    n_e, nf, dim, _ = wg.shape
    cap = x_rows.shape[ONE]
    list_rows = 2 * cap + 4 * GR
    n_in = ZERO if lists is None else 3

    def body(tab_ref, x_ref, wg_ref, wd_ref, bg_ref, bd_ref, *refs):
        refs = refs[n_in:]
        h_ref, a_ref, keep_ref, main_ref, over_ref, acc, h_st, a_st, p_st, pend, h_sem, a_sem, p_sem = refs
        e = pl.program_id(ZERO)
        f = pl.program_id(ONE)
        expert = e + 2 * half

        def wait_p(slot):
            def one(_, c):
                pltpu.make_async_copy(p_st.at[ZERO, pl.ds(ZERO, GR)], keep_ref.at[pl.ds(ZERO, GR)], p_sem.at[slot]).wait()
                return c

            lax.fori_loop(ZERO, pend[2 + slot], one, ZERO)
            pend[2 + slot] = ZERO

        def wait_ha(slot):
            @pl.when(pend[slot] == ONE)
            def _():
                pltpu.make_async_copy(h_st.at[ZERO], h_ref.at[ZERO, pl.ds(ZERO, BLK), pl.ds(ZERO, 2 * FT)], h_sem.at[slot]).wait()
                pltpu.make_async_copy(a_st.at[ZERO], a_ref.at[ZERO, pl.ds(ZERO, BLK), pl.ds(ZERO, FT)], a_sem.at[slot]).wait()
                pend[slot] = ZERO

        @pl.when((e == ZERO) & (f == ZERO))
        def _():
            for i in range(4):
                pend[i] = ZERO

        def block(i, m):
            r0 = mult(i * BLK, BLK)
            rows = pl.ds(r0, m)
            slot = lax.rem(i, 2)
            h = dot(x_ref[ZERO, rows, :], wg_ref[ZERO, ZERO]) + bg_ref[ZERO, ZERO]
            _, _, g, u1, s = swiglu_parts(h)
            a = (g * s * u1).astype(BF16)
            part = dot(a, wd_ref[ZERO])
            wait_ha(slot)
            h_st[slot, :m] = h
            a_st[slot, :m] = a
            pltpu.make_async_copy(h_st.at[slot], h_ref.at[e, pl.ds(r0, BLK), pl.ds(mult(f * 2 * FT, 2 * FT), 2 * FT)], h_sem.at[slot]).start()
            pltpu.make_async_copy(a_st.at[slot], a_ref.at[e, pl.ds(r0, BLK), pl.ds(mult(f * FT, FT), FT)], a_sem.at[slot]).start()
            pend[slot] = ONE

            @pl.when(f == ZERO)
            def _():
                acc[rows, :] = part

            @pl.when((f > ZERO) & (f < nf - ONE))
            def _():
                acc[rows, :] = acc[rows, :] + part

            @pl.when(f == nf - ONE)
            def _():
                wait_p(slot)
                p_st[slot, :m] = (acc[rows, :] + part + bd_ref[ZERO]).astype(BF16)
                end = tab_ref[tab.end + expert]
                mid = tab_ref[tab.mid + expert]
                seg = tab_ref[tab.seg]
                n = jnp.clip((end - r0 + GR - ONE) // GR, ZERO, m // GR)

                def send(k, c):
                    r = r0 + k * GR
                    in1 = (r >= mid).astype(I32)
                    to = jnp.where(in1 == ONE, tab_ref[tab.list1 + expert] + r - mid, tab_ref[tab.list0 + expert] + r)
                    src = p_st.at[slot, pl.ds(mult(k * GR, GR), GR)]

                    @pl.when(in1 == seg)
                    def _():
                        pltpu.make_async_copy(src, keep_ref.at[pl.ds(mult(to, GR), GR)], p_sem.at[slot]).start()

                    @pl.when((in1 != seg) & (to < main_rows))
                    def _():
                        pltpu.make_async_copy(src, main_ref.at[pl.ds(mult(to, GR), GR)], p_sem.at[slot]).start()

                    @pl.when((in1 != seg) & (to >= main_rows))
                    def _():
                        pltpu.make_async_copy(src, over_ref.at[pl.ds(mult(to - main_rows, GR), GR)], p_sem.at[slot]).start()

                    return c

                lax.fori_loop(ZERO, n, send, ZERO)
                pend[2 + slot] = n

        row_blocks(tab_ref, tab, expert, block)

        @pl.when((e == n_e - ONE) & (f == nf - ONE))
        def _():
            for slot in range(2):
                wait_ha(slot)
                wait_p(slot)

    any_spec = pl.BlockSpec(memory_space=pl.ANY)
    list_shapes = [jax.ShapeDtypeStruct((list_rows, dim), BF16), jax.ShapeDtypeStruct((main_rows, dim), BF16),
                   jax.ShapeDtypeStruct((list_rows - main_rows, dim), BF16)]
    return pl.pallas_call(
        body, name='expert_forward',
        grid_spec=pltpu.PrefetchScalarGridSpec(
            num_scalar_prefetch=ONE, grid=(n_e, nf),
            in_specs=[pl.BlockSpec((ONE, cap, dim), lambda e, f, t: (e + 2 * half, ZERO, ZERO), pipeline_mode=pl.Buffered(ONE)),
                      pl.BlockSpec((ONE, ONE, dim, 2 * FT), lambda e, f, t: (e, f, ZERO, ZERO)),
                      pl.BlockSpec((ONE, FT, dim), lambda e, f, t: (e, f, ZERO)),
                      pl.BlockSpec((ONE, ONE, ONE, 2 * FT), lambda e, f, t: (e, f, ZERO, ZERO)),
                      pl.BlockSpec((ONE, ONE, dim), lambda e, f, t: (e, ZERO, ZERO))] + [any_spec] * n_in,
            out_specs=[any_spec] * 5,
            scratch_shapes=[pltpu.VMEM((cap, dim), F32), pltpu.VMEM((2, BLK, 2 * FT), F32), pltpu.VMEM((2, BLK, FT), BF16),
                            pltpu.VMEM((2, BLK, dim), BF16), pltpu.SMEM((4,), I32),
                            pltpu.SemaphoreType.DMA((2,)), pltpu.SemaphoreType.DMA((2,)), pltpu.SemaphoreType.DMA((2,))]),
        out_shape=[jax.ShapeDtypeStruct((n_e, cap, nf * 2 * FT), F32), jax.ShapeDtypeStruct((n_e, cap, nf * FT), BF16)] + list_shapes,
        input_output_aliases={} if lists is None else {6: 2, 7: 3, 8: 4},
        compiler_params=params(2),
        cost_estimate=pl.CostEstimate(flops=6 * n_e * 1024 * dim * nf * FT, bytes_accessed=n_e * nf * dim * FT * 6, transcendentals=ZERO),
    )(vec, x_rows, wg, wd, bg, bd, *([] if lists is None else lists))


def expert_backward(vec, d_rows, wg, wd, bd, h_all, half, tab):
    n_e, nf, dim, _ = wg.shape
    cap = d_rows.shape[ONE]

    def body(tab_ref, d_ref, wg_ref, wd_ref, bd_ref, h_ref, dh_ref, dx_ref, g_ref, sbg_ref, sbd_ref,
             acc, gacc, h_buf, dh_st, dx_st, g_st, state, h_sem, dh_sem, o_sem):
        e = pl.program_id(ZERO)
        f = pl.program_id(ONE)
        expert = e + 2 * half

        def load(to_slot, ee, ff, i):
            return pltpu.make_async_copy(
                h_ref.at[ee, pl.ds(mult(i * BLK, BLK), BLK), pl.ds(mult(ff * 2 * FT, 2 * FT), 2 * FT)], h_buf.at[to_slot], h_sem.at[to_slot])

        def wait_dh(slot):
            @pl.when(state[ONE + slot] == ONE)
            def _():
                pltpu.make_async_copy(dh_st.at[ZERO], dh_ref.at[ZERO, pl.ds(ZERO, BLK), pl.ds(ZERO, 2 * FT)], dh_sem.at[slot]).wait()
                state[ONE + slot] = ZERO

        def wait_out(slot):
            @pl.when(state[3 + slot] == ONE)
            def _():
                pltpu.make_async_copy(dx_st.at[ZERO], dx_ref.at[ZERO, pl.ds(ZERO, BLK)], o_sem.at[slot]).wait()
                pltpu.make_async_copy(g_st.at[ZERO], g_ref.at[ZERO, pl.ds(ZERO, BLK)], o_sem.at[2 + slot]).wait()
                state[3 + slot] = ZERO

        @pl.when((e == ZERO) & (f == ZERO))
        def _():
            for i in range(5):
                state[i] = ZERO
            load(ZERO, ZERO, ZERO, ZERO).start()

        sbg_ref[...] = jnp.zeros_like(sbg_ref)

        @pl.when(f == ZERO)
        def _():
            sbd_ref[...] = jnp.zeros_like(sbd_ref)

        n_blocks = (tab_ref[tab.cover + expert] + BLK - ONE) // BLK

        def block(i, m):
            r0 = mult(i * BLK, BLK)
            rows = pl.ds(r0, m)
            slot = lax.rem(state[ZERO], 2)
            state[ZERO] = state[ZERO] + ONE
            load(slot, ZERO, ZERO, ZERO).wait()

            more = i + ONE < n_blocks
            next_f = f + ONE < nf

            @pl.when(more)
            def _():
                load(ONE - slot, e, f, i + ONE).start()

            @pl.when(jnp.logical_not(more) & (next_f | (e + ONE < n_e)))
            def _():
                load(ONE - slot, jnp.where(next_f, e, e + ONE), jnp.where(next_f, f + ONE, ZERO), ZERO).start()

            d = d_ref[ZERO, rows, :]
            da = dot_nt(d, wd_ref[ZERO])
            gate, up, g, u1, s = swiglu_parts(h_buf[slot, :m])
            gs = g * s
            a = (gs * u1).astype(BF16).astype(F32)
            pass_g = jnp.where(gate < LIMIT, 1.0, jnp.where(gate == LIMIT, 0.5, 0.0))
            pass_u = jnp.where(jnp.abs(up) < LIMIT, 1.0, jnp.where(jnp.abs(up) == LIMIT, 0.5, 0.0))
            dg = da * pass_g * (u1 * (s + ALPHA * gs * (1.0 - s)))
            du = da * pass_u * gs
            sbg_ref[ZERO, ZERO, :, :FT] += jnp.sum(dg, axis=ZERO, keepdims=True)
            sbg_ref[ZERO, ZERO, :, FT:] += jnp.sum(du, axis=ZERO, keepdims=True)
            prod = a * da
            gpart = sum(prod[:, LANES * q:LANES * q + LANES] for q in range(FT // LANES))
            dh = jnp.concatenate([dg.astype(BF16), du.astype(BF16)], axis=ONE)
            wait_dh(slot)
            dh_st[slot, :m] = dh
            pltpu.make_async_copy(dh_st.at[slot], dh_ref.at[e, pl.ds(r0, BLK), pl.ds(mult(f * 2 * FT, 2 * FT), 2 * FT)], dh_sem.at[slot]).start()
            state[ONE + slot] = ONE
            part = dot_nt(dh, wg_ref[ZERO, ZERO])

            @pl.when(f == ZERO)
            def _():
                d32 = d.astype(F32)
                sbd_ref[ZERO] += jnp.sum(d32, axis=ZERO, keepdims=True)
                db = d32 * bd_ref[ZERO]
                gacc[rows, :] = gpart + sum(db[:, LANES * q:LANES * q + LANES] for q in range(dim // LANES))
                acc[rows, :] = part

            @pl.when((f > ZERO) & (f < nf - ONE))
            def _():
                gacc[rows, :] = gacc[rows, :] + gpart
                acc[rows, :] = acc[rows, :] + part

            @pl.when(f == nf - ONE)
            def _():
                wait_out(slot)
                dx_st[slot, :m] = (acc[rows, :] + part).astype(BF16)
                total = jnp.sum(gacc[rows, :] + gpart, axis=ONE, keepdims=True)
                hi = total.astype(BF16).astype(F32)
                rest = total - hi
                mid = rest.astype(BF16).astype(F32)
                lane = lax.broadcasted_iota(I32, (m, LANES), ONE)
                g_st[slot, :m] = jnp.where(lane == ZERO, hi, jnp.where(lane == ONE, mid, jnp.where(lane == 2, rest - mid, 0.0))).astype(BF16)
                pltpu.make_async_copy(dx_st.at[slot], dx_ref.at[e, pl.ds(r0, BLK)], o_sem.at[slot]).start()
                pltpu.make_async_copy(g_st.at[slot], g_ref.at[e, pl.ds(r0, BLK)], o_sem.at[2 + slot]).start()
                state[3 + slot] = ONE

        row_blocks(tab_ref, tab, expert, block)

        @pl.when((e == n_e - ONE) & (f == nf - ONE))
        def _():
            for slot in range(2):
                wait_dh(slot)
                wait_out(slot)

    any_spec = pl.BlockSpec(memory_space=pl.ANY)
    return pl.pallas_call(
        body, name='expert_backward',
        grid_spec=pltpu.PrefetchScalarGridSpec(
            num_scalar_prefetch=ONE, grid=(n_e, nf),
            in_specs=[pl.BlockSpec((ONE, cap, dim), lambda e, f, t: (e + 2 * half, ZERO, ZERO), pipeline_mode=pl.Buffered(ONE)),
                      pl.BlockSpec((ONE, ONE, dim, 2 * FT), lambda e, f, t: (e, f, ZERO, ZERO)),
                      pl.BlockSpec((ONE, FT, dim), lambda e, f, t: (e, f, ZERO)),
                      pl.BlockSpec((ONE, ONE, dim), lambda e, f, t: (e, ZERO, ZERO)),
                      any_spec],
            out_specs=[any_spec, any_spec, any_spec,
                       pl.BlockSpec((ONE, ONE, ONE, 2 * FT), lambda e, f, t: (e, f, ZERO, ZERO)),
                       pl.BlockSpec((ONE, ONE, dim), lambda e, f, t: (e, ZERO, ZERO))],
            scratch_shapes=[pltpu.VMEM((cap, dim), F32), pltpu.VMEM((cap, LANES), F32), pltpu.VMEM((2, BLK, 2 * FT), F32),
                            pltpu.VMEM((2, BLK, 2 * FT), BF16), pltpu.VMEM((2, BLK, dim), BF16), pltpu.VMEM((2, BLK, LANES), BF16),
                            pltpu.SMEM((5,), I32), pltpu.SemaphoreType.DMA((2,)), pltpu.SemaphoreType.DMA((2,)), pltpu.SemaphoreType.DMA((4,))]),
        out_shape=[jax.ShapeDtypeStruct((n_e, cap, nf * 2 * FT), BF16), jax.ShapeDtypeStruct((n_e, cap, dim), BF16),
                   jax.ShapeDtypeStruct((n_e, cap, LANES), BF16), jax.ShapeDtypeStruct((n_e, nf, ONE, 2 * FT), F32),
                   jax.ShapeDtypeStruct((n_e, ONE, dim), F32)],
        compiler_params=params(2),
        cost_estimate=pl.CostEstimate(flops=6 * n_e * 1024 * dim * nf * FT, bytes_accessed=n_e * nf * dim * FT * 6, transcendentals=ZERO),
    )(vec, d_rows, wg, wd, bd, h_all)


def weight_grads(vec, x_rows, d_rows, dh, a, half, tab, other=None, width=None):
    n_e, cap, wide = dh.shape
    dim = x_rows.shape[2]
    nf = wide // (2 * FT)
    mrows = dim // MT

    def body(tab_ref, x_ref, d_ref, dh_ref, a_ref, *refs):
        if other is not None:
            rg_ref, rd_ref = refs[:2]
            refs = refs[2:]
        og_ref, od_ref, x_t, a_t, acc_g, acc_d = refs
        f = pl.program_id(ONE)
        part = pl.program_id(2)
        cover = tab_ref[tab.cover + pl.program_id(ZERO) + 2 * half]
        cols = pl.ds(mult(part * mrows, LANES), mrows)

        @pl.when(f == ZERO)
        def _():
            def turn(k, c):
                rows = pl.ds(mult(k * LANES, LANES), LANES)
                x_t[cols, rows] = x_ref[ZERO, rows, cols].T
                return c

            lax.fori_loop(ZERO, cover // LANES, turn, ZERO)

        @pl.when(part == ZERO)
        def _():
            def turn(k, c):
                rows = pl.ds(mult(k * LANES, LANES), LANES)
                a_t[:, rows] = a_ref[ZERO, rows, :].T
                return c

            lax.fori_loop(ZERO, cover // LANES, turn, ZERO)

        acc_g[...] = jnp.zeros_like(acc_g)
        acc_d[...] = jnp.zeros_like(acc_d)

        def chunk(start, size):
            rows = pl.ds(mult(start, LANES), size)
            acc_g[...] += dot(x_t[cols, rows], dh_ref[ZERO, rows, :])
            acc_d[...] += dot(a_t[:, rows], d_ref[ZERO, rows, cols])

        n_big = cover // 512

        def big(k, c):
            chunk(k * 512, 512)
            return c

        lax.fori_loop(ZERO, n_big, big, ZERO)

        @pl.when(cover % 512 >= 256)
        def _():
            chunk(n_big * 512, 256)

        @pl.when(cover % 256 >= LANES)
        def _():
            chunk(cover - LANES, LANES)

        if other is None:
            og_ref[ZERO, ZERO] = acc_g[...].astype(BF16)
            od_ref[ZERO] = acc_d[...].astype(BF16)
        else:
            od_ref[ZERO] = (acc_d[...] + rd_ref[ZERO].astype(F32)).astype(BF16)
            mat = pair_matrix_t()
            for g in range(2 * FT // 256):
                lo, hi = pl.ds(LANES * g, LANES), pl.ds(FT + LANES * g, LANES)
                gate = (acc_g[:, lo] + rg_ref[ZERO, ZERO, :, lo].astype(F32)).astype(BF16)
                up = (acc_g[:, hi] + rg_ref[ZERO, ZERO, :, hi].astype(F32)).astype(BF16)
                og_ref[ZERO, :, 256 * g:256 * g + 256] = dot(jnp.concatenate([gate, up], axis=ONE), mat).astype(BF16)

    tile_g = pl.BlockSpec((ONE, ONE, mrows, 2 * FT), lambda e, f, m, t: (e, f, m, ZERO))
    tile_d = pl.BlockSpec((ONE, FT, mrows), lambda e, f, m, t: (e, f, m))
    if other is None:
        out_specs = [tile_g, tile_d]
        out_shape = [jax.ShapeDtypeStruct((n_e, nf, dim, 2 * FT), BF16), jax.ShapeDtypeStruct((n_e, nf * FT, dim), BF16)]
        extra = []
    else:
        out_specs = [pl.BlockSpec((ONE, mrows, 2 * FT), lambda e, f, m, t: (e, m, f)), tile_d]
        out_shape = [jax.ShapeDtypeStruct((n_e, dim, width), BF16), jax.ShapeDtypeStruct((n_e, width // 2, dim), BF16)]
        extra = [tile_g, tile_d]
    whole = pl.BlockSpec((ONE, cap, dim), lambda e, f, m, t: (e + 2 * half, ZERO, ZERO), pipeline_mode=pl.Buffered(ONE))
    return pl.pallas_call(
        body, name='weight_grads',
        grid_spec=pltpu.PrefetchScalarGridSpec(
            num_scalar_prefetch=ONE, grid=(n_e, nf, MT),
            in_specs=[whole, whole,
                      pl.BlockSpec((ONE, cap, 2 * FT), lambda e, f, m, t: (e, ZERO, f)),
                      pl.BlockSpec((ONE, cap, FT), lambda e, f, m, t: (e, ZERO, f))] + extra,
            out_specs=out_specs,
            scratch_shapes=[pltpu.VMEM((dim, cap), BF16), pltpu.VMEM((FT, cap), BF16),
                            pltpu.VMEM((mrows, 2 * FT), F32), pltpu.VMEM((FT, mrows), F32)]),
        out_shape=out_shape,
        compiler_params=params(3),
        cost_estimate=pl.CostEstimate(flops=6 * n_e * 1024 * dim * nf * FT, bytes_accessed=n_e * nf * dim * FT * 6, transcendentals=ZERO),
    )(vec, x_rows, d_rows, dh, a, *([] if other is None else other))


def scatter_rows(vec, pos, dx_own, dx_oth, g_own, g_oth, tok, tab):
    dim = dx_own.shape[2]
    nw = tab.nw

    def body(tab_ref, pos_ref, xo_ref, xt_ref, go_ref, gt_ref, out_ref, gout_ref, fb, gb, acc, gacc, sem):
        w = pl.program_id(ZERO)
        slot = lax.rem(w, 2)

        def fetch(win, to):
            for e in range(4):
                at = e * nw + win
                src, gsrc = (xo_ref, go_ref) if e < 2 else (xt_ref, gt_ref)

                def one(k, c):
                    rows = pl.ds(mult(tab_ref[tab.first + at] + GR * k, GR), GR)
                    put = pl.ds(mult(tab_ref[tab.flat + at] + GR * k, GR), GR)
                    pltpu.make_async_copy(src.at[e % 2, rows], fb.at[to, put], sem.at[to]).start()
                    pltpu.make_async_copy(gsrc.at[e % 2, rows], gb.at[to, put], sem.at[2 + to]).start()
                    return c

                lax.fori_loop(ZERO, tab_ref[tab.count + at], one, ZERO)

        @pl.when(w == ZERO)
        def _():
            fb[...] = jnp.zeros_like(fb)
            gb[...] = jnp.zeros_like(gb)
            fetch(ZERO, ZERO)

        @pl.when(w + ONE < nw)
        def _():
            fetch(w + ONE, ONE - slot)

        def one_wait(k, c):
            pltpu.make_async_copy(xo_ref.at[ZERO, pl.ds(ZERO, GR)], fb.at[slot, pl.ds(ZERO, GR)], sem.at[slot]).wait()
            pltpu.make_async_copy(go_ref.at[ZERO, pl.ds(ZERO, GR)], gb.at[slot, pl.ds(ZERO, GR)], sem.at[2 + slot]).wait()
            return c

        lax.fori_loop(ZERO, sum(tab_ref[tab.count + e * nw + w] for e in range(4)), one_wait, ZERO)

        acc[...] = jnp.zeros_like(acc)
        gacc[...] = jnp.zeros_like(gacc)

        def block(b, c):
            j = lax.broadcasted_iota(I32, (BLK, WIN), ZERO) + b * BLK
            m0 = pos_ref[ZERO:ONE, :] == j
            m1 = pos_ref[ONE:2, :] == j
            rows = pl.ds(mult(b * BLK, BLK), BLK)
            acc[...] += dot_tn(jnp.where(m0 | m1, 1.0, 0.0).astype(BF16), fb[slot, rows, :])
            gv = gb[slot, rows, :]
            gacc[ZERO] += dot_tn(jnp.where(m0, 1.0, 0.0).astype(BF16), gv)
            gacc[ONE] += dot_tn(jnp.where(m1, 1.0, 0.0).astype(BF16), gv)
            return c

        lax.fori_loop(ZERO, flat_blocks(tab_ref, tab, w), block, ZERO)
        out_ref[...] = acc[...].astype(BF16)
        lane = lax.broadcasted_iota(I32, (WIN, LANES), ONE)
        g0 = jnp.sum(gacc[ZERO], axis=ONE, keepdims=True)
        g1 = jnp.sum(gacc[ONE], axis=ONE, keepdims=True)
        gout_ref[...] = jnp.where(lane == ZERO, g0, jnp.where(lane == ONE, g1, 0.0))

    any_spec = pl.BlockSpec(memory_space=pl.ANY)
    return pl.pallas_call(
        body, name='scatter_rows',
        grid_spec=pltpu.PrefetchScalarGridSpec(
            num_scalar_prefetch=ONE, grid=(nw,),
            in_specs=[pl.BlockSpec((2, WIN), lambda w, t: (ZERO, w))] + [any_spec] * 4,
            out_specs=[pl.BlockSpec((WIN, dim), lambda w, t: (w, ZERO)), pl.BlockSpec((WIN, LANES), lambda w, t: (w, ZERO))],
            scratch_shapes=[pltpu.VMEM((2, FLAT, dim), BF16), pltpu.VMEM((2, FLAT, LANES), BF16), pltpu.VMEM((WIN, dim), F32),
                            pltpu.VMEM((2, WIN, LANES), F32), pltpu.SemaphoreType.DMA((4,))]),
        out_shape=[jax.ShapeDtypeStruct((tok, dim), BF16), jax.ShapeDtypeStruct((tok, LANES), F32)],
        compiler_params=params(ONE),
        cost_estimate=pl.CostEstimate(flops=8 * tok * 256 * dim, bytes_accessed=4 * tok * dim, transcendentals=ZERO),
    )(vec, pos, dx_own, dx_oth, g_own, g_oth)


def combine_rows(vec, pos, tok_w, keep, r_main, r_over, own, tab):
    dim = keep.shape[ONE]
    nw = tab.nw
    per = nw // 4
    main_rows = r_main.shape[ZERO]

    def window(i, t):
        px = t[tab.x] if own else ONE - t[tab.x]
        return t[tab.seg] * (nw // 2) + px * per + i

    def body(tab_ref, pos_ref, w_ref, keep_ref, main_ref, over_ref, out_ref, kb, rb, acc, sem):
        i = pl.program_id(ZERO)
        slot = lax.rem(i, 2)
        seg = tab_ref[tab.seg]

        def fetch(step, to):
            win = window(step, tab_ref)
            for e in range(4):
                at = e * nw + win
                shift = jnp.where(seg == ONE, tab_ref[tab.list1 + e] - tab_ref[tab.mid + e], tab_ref[tab.list0 + e])

                def one(k, c):
                    row = tab_ref[tab.first + at] + shift + GR * k
                    put = pl.ds(mult(tab_ref[tab.flat + at] + GR * k, GR), GR)
                    pltpu.make_async_copy(keep_ref.at[pl.ds(mult(row, GR), GR)], kb.at[to, put], sem.at[to]).start()

                    @pl.when(row < main_rows)
                    def _():
                        pltpu.make_async_copy(main_ref.at[pl.ds(mult(row, GR), GR)], rb.at[to, put], sem.at[2 + to]).start()

                    @pl.when(row >= main_rows)
                    def _():
                        pltpu.make_async_copy(over_ref.at[pl.ds(mult(row - main_rows, GR), GR)], rb.at[to, put], sem.at[2 + to]).start()

                    return c

                lax.fori_loop(ZERO, tab_ref[tab.count + at], one, ZERO)

        @pl.when(i == ZERO)
        def _():
            kb[...] = jnp.zeros_like(kb)
            rb[...] = jnp.zeros_like(rb)
            fetch(ZERO, ZERO)

        @pl.when(i + ONE < per)
        def _():
            fetch(i + ONE, ONE - slot)

        w = window(i, tab_ref)

        def one_wait(k, c):
            pltpu.make_async_copy(keep_ref.at[pl.ds(ZERO, GR)], kb.at[slot, pl.ds(ZERO, GR)], sem.at[slot]).wait()
            pltpu.make_async_copy(main_ref.at[pl.ds(ZERO, GR)], rb.at[slot, pl.ds(ZERO, GR)], sem.at[2 + slot]).wait()
            return c

        lax.fori_loop(ZERO, sum(tab_ref[tab.count + e * nw + w] for e in range(4)), one_wait, ZERO)

        acc[...] = jnp.zeros_like(acc)

        def block(b, c):
            j = lax.broadcasted_iota(I32, (BLK, WIN), ZERO) + b * BLK
            rows = pl.ds(mult(b * BLK, BLK), BLK)
            y = (kb[slot, rows, :].astype(F32) + rb[slot, rows, :].astype(F32)).astype(BF16)
            acc[ZERO] += dot_tn(jnp.where(pos_ref[ZERO:ONE, :] == j, 1.0, 0.0).astype(BF16), y)
            acc[ONE] += dot_tn(jnp.where(pos_ref[ONE:2, :] == j, 1.0, 0.0).astype(BF16), y)
            return c

        lax.fori_loop(ZERO, flat_blocks(tab_ref, tab, w), block, ZERO)
        w0, w1, both = w_ref[:, ZERO:ONE], w_ref[:, ONE:2], w_ref[:, 2:3]
        out_ref[...] = jnp.where(both > 0.5, w0 * acc[ZERO] + w1 * acc[ONE], acc[ZERO] + acc[ONE]).astype(BF16)

    any_spec = pl.BlockSpec(memory_space=pl.ANY)
    return pl.pallas_call(
        body, name='combine_rows',
        grid_spec=pltpu.PrefetchScalarGridSpec(
            num_scalar_prefetch=ONE, grid=(per,),
            in_specs=[pl.BlockSpec((2, WIN), lambda i, t: (ZERO, window(i, t))),
                      pl.BlockSpec((WIN, 8), lambda i, t: (window(i, t), ZERO)), any_spec, any_spec, any_spec],
            out_specs=pl.BlockSpec((WIN, dim), lambda i, t: (i, ZERO)),
            scratch_shapes=[pltpu.VMEM((2, FLAT, dim), BF16), pltpu.VMEM((2, FLAT, dim), BF16), pltpu.VMEM((2, WIN, dim), F32),
                            pltpu.SemaphoreType.DMA((4,))]),
        out_shape=jax.ShapeDtypeStruct((per * WIN, dim), BF16),
        compiler_params=params(ONE),
        cost_estimate=pl.CostEstimate(flops=4 * per * WIN * 512 * dim, bytes_accessed=6 * per * WIN * dim, transcendentals=ZERO),
    )(vec, pos, tok_w, keep, r_main, r_over)


def solution(mesh):
    tp_n, ep_n = mesh.shape['tp'], mesh.shape['ep']
    fine = Mesh(mesh.devices.reshape(tp_n, ep_n // 2, 2), ('tp', 'x', 'c'))
    group = ('tp', 'x')
    every = ('tp', 'x', 'c')
    swap = [(ZERO, ONE), (ONE, ZERO)]

    def device_fn(x_loc, idx_loc, slot_loc, w_router, b_router, w_gu, b_gu, w_dn, b_dn, dy_loc):
        n_tok, dim = x_loc.shape
        n_experts = w_router.shape[ONE]
        n_loc, _, width = w_gu.shape
        units = width // 2
        nf = pl.cdiv(units, FT)
        tok = 4 * n_tok
        cap = 4 * (2 * n_tok * 2 // n_experts)
        tab = Table(tok // WIN)
        main_rows = cap
        tp_pos, x_pos, c_pos = lax.axis_index('tp'), lax.axis_index('x'), lax.axis_index('c')

        logits = jnp.dot(x_loc, w_router, preferred_element_type=F32) + b_router[None, :]
        hot = idx_loc[:, :, None] == jnp.arange(n_experts)[None, None, :]
        picked = jnp.sum(jnp.where(hot, logits[:, None, :], 0.0), axis=2)
        gate_w = jax.nn.softmax(picked, axis=ONE)
        mine = jnp.concatenate([idx_loc.astype(F32), slot_loc.astype(F32), gate_w, jnp.zeros((n_tok, 2), F32)], axis=ONE)
        shared = lax.all_gather(mine.T, group, axis=ZERO)
        shared = shared.transpose(ONE, ZERO, 2).reshape(8, tok)
        x_all = lax.all_gather(x_loc, group, axis=ZERO, tiled=True)
        d_all = lax.all_gather(dy_loc, group, axis=ZERO, tiled=True)
        idx_t, slot_t, w_t = shared[ZERO:2].astype(I32), shared[2:4].astype(I32), shared[4:6]
        vec, pos, totals = make_table(idx_t, slot_t, x_pos, c_pos, tp_pos, tab)
        most = lax.pmax(jnp.max(totals), every)
        vec, most = lax.optimization_barrier((vec, most))
        spill = most > main_rows
        both_t = ((pos[ZERO] >= ZERO) & (pos[ONE] >= ZERO)).astype(F32)
        tok_w = jnp.concatenate([w_t, both_t[None], jnp.zeros((5, tok), F32)], axis=ZERO).T

        wg = (split_weights(w_gu),)
        wd = (jnp.pad(w_dn, ((ZERO, ZERO), (ZERO, nf * FT - units), (ZERO, ZERO))),)
        bg = jnp.pad(b_gu.reshape(n_loc, units, 2), ((ZERO, ZERO), (ZERO, nf * FT - units), (ZERO, ZERO)))
        bg = bg.reshape(n_loc, nf, FT, 2).transpose(ZERO, ONE, 3, 2).reshape(n_loc, nf, ONE, 2 * FT)
        bd = jnp.where(tp_pos == ZERO, b_dn, 0.0).reshape(n_loc, ONE, dim)
        trade = functools.partial(lax.ppermute, axis_name='c', perm=swap)
        wg += (trade(wg[ZERO]),)
        wd += (trade(wd[ZERO]),)
        bg = (bg, trade(bg))
        bd = (bd, trade(bd))

        x_rows = gather_rows(vec, pos, x_all, cap, tab)
        h0, a0, *lists = expert_forward(vec, x_rows, wg[ZERO], wd[ZERO], bg[ZERO], bd[ZERO], ZERO, None, main_rows, tab)
        h1, a1, *lists = expert_forward(vec, x_rows, wg[ONE], wd[ONE], bg[ONE], bd[ONE], ONE, lists, main_rows, tab)
        keep, s_main, s_over = lists
        other_tp = functools.partial(lax.ppermute, axis_name='tp', perm=swap)
        r_main = other_tp(s_main)
        r_over = lax.cond(spill, other_tp, lambda b: b, s_over)

        d_rows = gather_rows(vec, pos, d_all, cap, tab, w_t)
        dh1, dx1, g1, sbg1, sbd1 = expert_backward(vec, d_rows, wg[ONE], wd[ONE], bd[ONE], h1, ONE, tab)
        part_g, part_d = weight_grads(vec, x_rows, d_rows, dh1, a1, ONE, tab)
        back_g, back_d = trade(part_g), trade(part_d)
        y_out = combine_rows(vec, pos, tok_w, keep, r_main, r_over, False, tab)
        y_in = lax.ppermute(y_out, 'x', swap)
        dh0, dx0, g0, sbg0, sbd0 = expert_backward(vec, d_rows, wg[ZERO], wd[ZERO], bd[ZERO], h0, ZERO, tab)
        dx_tok, g_tok = scatter_rows(vec, pos, dx0, dx1, g0, g1, tok, tab)
        g_sum = lax.psum_scatter(g_tok, group, scatter_dimension=ZERO, tiled=True)[:, :2]
        dx_sum = lax.psum_scatter(dx_tok, group, scatter_dimension=ZERO, tiled=True)
        grad_w_gu, grad_w_dn = weight_grads(vec, x_rows, d_rows, dh0, a0, ZERO, tab, (back_g, back_d), width)

        y_own = combine_rows(vec, pos, tok_w, keep, r_main, r_over, True, tab)
        kept = slot_loc >= ZERO
        here = idx_loc // 4 == x_pos
        y_k = jnp.where(here[:, :, None], y_own.astype(F32)[:, None, :], y_in.astype(F32)[:, None, :])
        y_sum = jnp.sum(jnp.where(kept[:, :, None], gate_w[:, :, None] * y_k, 0.0), axis=ONE).astype(BF16)
        all_here = jnp.all(kept & here, axis=ONE, keepdims=True)
        all_there = jnp.all(kept & ~here, axis=ONE, keepdims=True)
        moe_out = jnp.where(all_here, y_own, jnp.where(all_there, y_in, y_sum))

        d_picked = g_sum - gate_w * jnp.sum(g_sum, axis=ONE, keepdims=True)
        d_logits = jnp.sum(jnp.where(hot, d_picked[:, :, None], 0.0), axis=ONE)
        d_logits_b = d_logits.astype(BF16)
        grad_w_router = lax.psum(jnp.einsum('td,te->de', x_loc, d_logits_b, preferred_element_type=F32), every)
        grad_b_router = lax.psum(jnp.sum(d_logits, axis=ZERO), every)
        grad_x = (dx_sum.astype(F32) + jnp.einsum('te,de->td', d_logits_b, w_router, preferred_element_type=F32)).astype(BF16)

        sbg = sbg0 + trade(sbg1)
        grad_b_gu = sbg.reshape(n_loc, nf, 2, FT).transpose(ZERO, ONE, 3, 2).reshape(n_loc, nf * FT * 2)[:, :width]
        grad_b_dn = (sbd0 + trade(sbd1)).reshape(n_loc, dim)
        return (moe_out, grad_x, grad_w_gu, grad_b_gu, grad_w_dn, grad_b_dn, grad_w_router, grad_b_router)

    ep = ('x', 'c')
    toks = P(('x', 'c', 'tp'), None)
    in_specs = (toks, toks, toks, P(None, None), P(None), P(ep, None, 'tp'), P(ep, 'tp'), P(ep, 'tp', None), P(ep, None), toks)
    out_specs = (toks, toks, P(ep, None, 'tp'), P(ep, 'tp'), P(ep, 'tp', None), P(ep, None), P(None, None), P(None))

    return jax.shard_map(device_fn, mesh=fine, in_specs=in_specs, out_specs=out_specs, check_vma=False)
```

time: 4100 us -> 2060 us (0.50)
  the two profiles are of different devices: /device:TPU:0 before, /device:TPU:7 now
where the time goes in v1:
time: 2060 us; the launch traced here: 2050 us
  Pallas kernels  1170 us (57%)
  waiting for transfers between devices  371 us (18%)
  blocking collectives  214 us (10%)
  starting transfers between devices  198 us (10%)
  local copies, waits for them, and re-layouts  40.9 us (2%)
  other arithmetic  31 us (2%)
    ppermute x1, waiting for transfers between devices, device_fn(): r_main = other_tp(s_main)  369 us
    pallas_call x2, Pallas kernels, weight_grads(): pl.pallas_call(body, name='weight_grads', grid_spec=pltpu.PrefetchScalarG...  364 us
    pallas_call x2, Pallas kernels, expert_backward(): pl.pallas_call(body, name='expert_backward', grid_spec=pltpu.PrefetchScal...  360 us
    pallas_call x2, Pallas kernels, expert_forward(): pl.pallas_call(body, name='expert_forward', grid_spec=pltpu.PrefetchScala...  277 us
    ppermute x2, starting transfers between devices, device_fn(): back_g, back_d = (trade(part_g), trade(part_d))  193 us
    psum x1, blocking collectives, device_fn(): grad_b_router = lax.psum(jnp.sum(d_logits, axis=ZERO), every)  112 us
    pmax x1, blocking collectives, device_fn(): most = lax.pmax(jnp.max(totals), every)  94.8 us
    pallas_call x1, Pallas kernels, split_weights(): pl.pallas_call(body, name='split_weights', grid=(n_e, nf, MT), in_specs=[...  57.3 us
  transfers between devices with their start and end apart: 15, of which 2 were waited for; matrix products, arithmetic and copies ran while one was open for 4% of the time, Pallas kernels for 39%

profile of v1, /device:TPU:7, one launch (start us, length us, event | category | flops | bytes accessed | tf_op | source)
XLA Modules:
  0.0 2053.8 jit_solution(13119462495064911037)
XLA Ops:
  7.2 0.7 all-gather.4.cloned.1.call-update
  8.0 57.3 %split_weights.1.wg_ref = bf16[2,6,2304,1024]{3,2,1,0:T(8,128)(2,1)} custom-call(bf16[2,2304,5760]{2,1,0:T(8,128)(2,1)} %w_ref.1), custom_call_target="tpu_custom_call" | custom-call | flops 13589544960 | bytes 106168320 | tf_op jit(solution)/shard_map/split_weights/pallas_call | solution.py:144
  65.3 0.7 collective-permute-start.1
  66.1 20.2 pad.8.wd_ref
  86.4 0.5 collective-permute-start.4
  87.0 3.6 convolution_add_fusion
  90.8 0.2 copy.139
  91.0 0.3 copy-done.11
  91.4 0.2 broadcast_divide_fusion
  91.6 0.2 copy.141
  91.9 7.7 all-gather
  99.6 0.6 fusion.43
  100.2 0.3 and_select_fusion.3
  100.7 0.2 fusion.36
  101.0 0.2 reduce_sum.87
  101.2 4.7 reshape.302
  105.8 2.0 pad.9
  107.9 1.2 copy.161
  109.2 0.6 reduce_max.28
  109.8 1.0 collective-permute-start.3
  110.8 94.8 %pmax.7 = s32[]{:T(128)} all-reduce(s32[]{:T(128)} %reduce_max.28), channel_id=1, replica_groups=mesh['tp'=2,'x'=2,'c'=2] {'tp','x','c'}, use_global_device_ids=true, to_apply=%region_11.12 | all-reduce | flops 1 | bytes 8 | tf_op jit(solution)/shard_map/pmax | solution.py:834
  205.9 0.2 fusion.8
  206.1 0.2 fusion
  206.8 0.3 copy.144
  207.2 0.2 reduce_window_sum.26
  207.9 0.2 slice_reduce_fusion.3
  208.1 0.2 slice_reduce_fusion.1
  208.4 0.7 concatenate.10.tab_ref
  209.5 0.8 select_reduce_fusion.1.refs_0_.pos_ref
  210.2 24.5 %gather_rows.2.x_ref = bf16[4,2048,2304]{2,1,0:T(8,128)(2,1)} custom-call(s32[342]{0:T(512)} %concatenate.10.tab_ref, s32[2,4096]{1,0:T(2,128)} %select_reduce_fusion.1.refs_0_.pos_ref, bf16[4096,2304]{1,0:T(8,128)(2,1)} %all-gather.4.cloned.1.call-done.refs_1_), custom_call_target="tpu_custom_call" | custom-call | flops 19327352832 | bytes 37748736 | tf_op jit(solution)/shard_map/gather_rows/pallas_call | solution.py:251
  234.8 181.6 %expert_forward.2 = (f32[2,2048,6144]{2,1,0:T(8,128)}, bf16[2,2048,3072]{2,1,0:T(8,128)(2,1)}, bf16[4160,2304]{1,0:T(8,128)(2,1)}, bf16[2048,2304]{1,0:T(8,128)(2,1)}, bf16[2112,2304]{1,0:T(8,128)(2,1)}) custom-call(s32[342]{0:T(512)} %concatenate.10.tab_ref, bf16[4,2048,2304]{2,1,0:T(8,128)(2,1)} %gather_rows.2.x_ref, ...), custom_call_target="tpu_custom_call" | custom-call | flops 86973087744 | bytes 84934656 | tf_op jit(solution)/shard_map/expert_forward/pallas_call | solution.py:387
  416.4 25.0 %gather_rows.3.d_ref = bf16[4,2048,2304]{2,1,0:T(8,128)(2,1)} custom-call(s32[342]{0:T(512)} %concatenate.10.tab_ref, s32[2,4096]{1,0:T(2,128)} %select_reduce_fusion.1.refs_0_.pos_ref, f32[2,4096]{1,0:T(2,128)} %bitcast.73, bf16[4096,2304]{1,0:T(8,128)(2,1)} %all-gather.6.cloned.1.call-done.refs_2_), custom_call_target="tpu_custom_call" | custom-call | flops 19327352832 | bytes 37748736 | tf_op jit(solution)/shard_map/gather_rows/pallas_call | solution.py:251
  441.5 0.6 copy-done.21
  442.1 95.1 %expert_forward.3 = (f32[2,2048,6144]{2,1,0:T(8,128)}, bf16[2,2048,3072]{2,1,0:T(8,128)(2,1)}, bf16[4160,2304]{1,0:T(8,128)(2,1)}, bf16[2048,2304]{1,0:T(8,128)(2,1)}, bf16[2112,2304]{1,0:T(8,128)(2,1)}) custom-call(s32[342]{0:T(512)} %concatenate.10.tab_ref, ...), custom_call_target="tpu_custom_call", output_to_operand_aliasing={{2}: (6, {}), {3}: (7, {}), {4}: (8, {})} | custom-call | flops 86973087744 | bytes 84934656 | tf_op jit(solution)/shard_map/expert_forward/pallas_call | solution.py:387
  537.2 131.4 %expert_backward.3 = (bf16[2,2048,6144]{2,1,0:T(8,128)(2,1)}, bf16[2,2048,2304]{2,1,0:T(8,128)(2,1)}, bf16[2,2048,128]{2,1,0:T(8,128)(2,1)}, f32[2,6,1,1024]{3,2,1,0:T(1,128)}, f32[2,1,2304]{2,1,0:T(1,128)}) custom-call(s32[342]{0:T(512)} %concatenate.10.tab_ref, bf16[4,2048,2304]{2,1,0:T(8,128)(2,1)} %gather_rows.3.d_ref, ...), custom_call_target="tpu_custom_call" | custom-call | flops 86973087744 | bytes 84934656 | tf_op jit(solution)/shard_map/expert_backward/pallas_call | solution.py:522
  668.6 134.7 %weight_grads.2 = (bf16[2,6,2304,1024]{3,2,1,0:T(8,128)(2,1)}, bf16[2,3072,2304]{2,1,0:T(8,128)(2,1)}) custom-call(s32[342]{0:T(512)} %concatenate.10.tab_ref, bf16[4,2048,2304]{2,1,0:T(8,128)(2,1)} %gather_rows.2.x_ref, bf16[4,2048,2304]{2,1,0:T(8,128)(2,1)} %gather_rows.3.d_ref, bf16[2,2048,6144]{2,1,0:T(8,128)(2,1)} %get-tuple-element.59.dh_ref, ...), custom_call_target="tpu_custom_call" | custom-call | flops 86973087744 | bytes 84934656 | tf_op jit(solution)/shard_map/weight_grads/pallas_call | solution.py:626
  803.3 192.8 %collective-permute-start.7 = (bf16[2,6,2304,1024]{3,2,1,0:T(8,128)(2,1)}, bf16[2,6,2304,1024]{3,2,1,0:T(8,128)(2,1)}, u32[]{:S(2)}, u32[]{:S(2)}) collective-permute-start(bf16[2,6,2304,1024]{3,2,1,0:T(8,128)(2,1)} %get-tuple-element.61), channel_id=1, source_target_pairs={{0,1},{1,0},{2,3},{3,2},{4,5},{5,4},{6,7},{7,6}} | collective-permute-start | bytes 169869312 | tf_op jit(solution)/shard_map/ppermute | solution.py:862
  996.0 229.1 %expert_backward.2 = (bf16[2,2048,6144]{2,1,0:T(8,128)(2,1)}, bf16[2,2048,2304]{2,1,0:T(8,128)(2,1)}, bf16[2,2048,128]{2,1,0:T(8,128)(2,1)}, f32[2,6,1,1024]{3,2,1,0:T(1,128)}, f32[2,1,2304]{2,1,0:T(1,128)}) custom-call(s32[342]{0:T(512)} %concatenate.10.tab_ref, bf16[4,2048,2304]{2,1,0:T(8,128)(2,1)} %gather_rows.3.d_ref, ...), custom_call_target="tpu_custom_call" | custom-call | flops 86973087744 | bytes 84934656 | tf_op jit(solution)/shard_map/expert_backward/pallas_call | solution.py:522
  1225.1 31.8 %scatter_rows.1 = (bf16[4096,2304]{1,0:T(8,128)(2,1)}, f32[4096,128]{1,0:T(8,128)}) custom-call(s32[342]{0:T(512)} %concatenate.10.tab_ref, s32[2,4096]{1,0:T(2,128)} %select_reduce_fusion.1.refs_0_.pos_ref, bf16[2,2048,2304]{2,1,0:T(8,128)(2,1)} %get-tuple-element.50.xo_ref, bf16[2,2048,2304]{2,1,0:T(8,128)(2,1)} %get-tuple-element.52.xt_ref, ...), custom_call_target="tpu_custom_call" | custom-call | flops 19327352832 | bytes 37748736 | tf_op jit(solution)/shard_map/scatter_rows/pallas_call | solution.py:703
  1257.0 0.5 reduce-scatter.3.cloned.1.call-update
  1257.6 1.2 collective-permute-start.5
  1259.6 1.9 copy.159
  1261.6 368.9 %collective-permute-done.5.main_ref = bf16[2048,2304]{1,0:T(8,128)(2,1)} collective-permute-done((bf16[2048,2304]{1,0:T(8,128)(2,1)}, bf16[2048,2304]{1,0:T(8,128)(2,1)}, u32[]{:S(2)}, u32[]{:S(2)}) %collective-permute-start.5) | collective-permute-done | bytes 9437216 | tf_op jit(solution)/shard_map/ppermute | solution.py:856
  1630.5 15.7 combine_rows.3
  1646.2 1.4 collective-permute-start.10
  1647.7 0.7 collective-permute-done.10
  1648.5 0.6 copy.183
  1649.3 1.1 copy.164
  1650.3 2.2 reshape.307
  1652.5 0.6 slice.66
  1653.1 1.2 slice_reduce_fusion
  1654.4 1.5 multiply_subtract_fusion
  1655.9 0.2 copy.163
  1656.3 111.7 %psum.15 = f32[8]{0:T(128)} all-reduce(f32[8]{0:T(128)S(1)} %get-tuple-element.69), channel_id=1, replica_groups=mesh['tp'=2,'x'=2,'c'=2] {'tp','x','c'}, use_global_device_ids=true, to_apply=%region_23.24 | all-reduce | flops 8 | bytes 64 | tf_op jit(solution)/shard_map/psum | solution.py:884
  1768.0 3.7 convolution_bitcast_fusion
  1771.7 5.2 fusion.44
  1776.9 15.5 combine_rows.2
  1792.3 3.0 convert_element_type.106
  1795.4 3.2 convert_element_type.107
  1798.7 4.8 select_reduce_fusion
  1803.5 4.7 select_select_fusion
  1808.1 8.2 add_convert_fusion
  1816.3 229.2 %weight_grads.3 = (bf16[2,2304,5760]{2,1,0:T(8,128)(2,1)}, bf16[2,2880,2304]{2,1,0:T(8,128)(2,1)}) custom-call(s32[342]{0:T(512)} %concatenate.10.tab_ref, bf16[4,2048,2304]{2,1,0:T(8,128)(2,1)} %gather_rows.2.x_ref, bf16[4,2048,2304]{2,1,0:T(8,128)(2,1)} %gather_rows.3.d_ref, bf16[2,2048,6144]{2,1,0:T(8,128)(2,1)} %get-tuple-element.57.dh_ref, ...), custom_call_target="tpu_custom_call" | custom-call | flops 86973087744 | bytes 84934656 | tf_op jit(solution)/shard_map/weight_grads/pallas_call | solution.py:626
  2045.5 1.5 copy.190
  (133 shorter events, 3.7 us)
Async XLA Ops:
  7.2 79.9 %copy-start = (bf16[2304,8]{0,1:T(8,128)(2,1)S(1)}, bf16[2304,8]{0,1:T(8,128)(2,1)}, u32[]{:S(2)}) copy-start(bf16[2304,8]{0,1:T(8,128)(2,1)} %param.15) | copy-start | bytes 110596
  7.2 203.0 %all-gather.4.cloned.1.call-start = ((), (), s32[]{:S(2)}) async-start(), calls=%async_computation.2 | async-start | bytes 23592960 | tf_op jit(solution)/shard_map/all_gather | solution.py:830
  7.9 408.5 %all-gather.6.cloned.1.call-start = ((), (), s32[]{:S(2)}) async-start(), calls=%async_computation.3 | async-start | bytes 23592960 | tf_op jit(solution)/shard_map/all_gather | solution.py:831
  65.3 376.2 %collective-permute-start.1 = (bf16[2,6,2304,1024]{3,2,1,0:T(8,128)(2,1)}, bf16[2,6,2304,1024]{3,2,1,0:T(8,128)(2,1)}, u32[]{:S(2)}, u32[]{:S(2)}) collective-permute-start(bf16[2,6,2304,1024]{3,2,1,0:T(8,128)(2,1)} %split_weights.1.wg_ref), channel_id=1, source_target_pairs={{0,1},{1,0},{2,3},{3,2},{4,5},{5,4},{6,7},{7,6}} | collective-permute-start | bytes 169869312 | tf_op jit(solution)/shard_map/ppermute | solution.py:846
  66.0 20.4 copy-start.16
  66.0 20.9 %copy-start.13 = (s32[1024,2]{0,1:T(2,128)S(1)}, s32[1024,2]{0,1:T(2,128)}, u32[]{:S(2)}) copy-start(s32[1024,2]{0,1:T(2,128)} %param.14) | copy-start | bytes 24580
  66.0 20.9 %copy-start.3 = (s32[1024,2]{0,1:T(2,128)S(1)}, s32[1024,2]{0,1:T(2,128)}, u32[]{:S(2)}) copy-start(s32[1024,2]{0,1:T(2,128)} %param.13) | copy-start | bytes 24580
  66.0 21.0 %copy-start.18 = (f32[8]{0:T(128)S(1)}, f32[8]{0:T(128)}, u32[]{:S(2)}) copy-start(f32[8]{0:T(128)} %param.16) | copy-start | bytes 100
  66.0 35.1 %copy-start.10 = (f32[2,5760]{1,0:T(2,128)S(1)}, f32[2,5760]{1,0:T(2,128)}, u32[]{:S(2)}) copy-start(f32[2,5760]{1,0:T(2,128)} %param.18) | copy-start | bytes 138244
  66.1 1587.1 %reduce-scatter.5.cloned.1.call-start = ((), (), s32[]{:S(2)}) async-start(), calls=%async_computation.5 | async-start | bytes 2621440 | tf_op jit(solution)/shard_map/reduce_scatter | solution.py:867
  86.3 355.1 %collective-permute-start.2 = (bf16[2,3072,2304]{2,1,0:T(8,128)(2,1)}, bf16[2,3072,2304]{2,1,0:T(8,128)(2,1)}, u32[]{:S(2)}, u32[]{:S(2)}) collective-permute-start(bf16[2,3072,2304]{2,1,0:T(8,128)(2,1)} %pad.8.wd_ref), channel_id=1, source_target_pairs={{0,1},{1,0},{2,3},{3,2},{4,5},{5,4},{6,7},{7,6}} | collective-permute-start | bytes 84934664 | tf_op jit(solution)/shard_map/ppermute | solution.py:847
  86.4 22.7 %copy-start.17 = (f32[2,1,2304]{2,1,0:T(1,128)}, f32[2,1,2304]{2,1,0:T(1,128)S(1)}, u32[]{:S(2)}) copy-start(f32[2,1,2304]{2,1,0:T(1,128)S(1)} %reshape.305.bd_ref) | copy-start | bytes 55300
  86.4 355.0 %collective-permute-start.4 = (f32[2,1,2304]{2,1,0:T(1,128)S(1)}, f32[2,1,2304]{2,1,0:T(1,128)S(1)}, u32[]{:S(2)}, u32[]{:S(2)}) collective-permute-start(f32[2,1,2304]{2,1,0:T(1,128)S(1)} %reshape.305.bd_ref), channel_id=1, source_target_pairs={{0,1},{1,0},{2,3},{3,2},{4,5},{5,4},{6,7},{7,6}} | collective-permute-start | bytes 55304 | tf_op jit(solution)/shard_map/ppermute | solution.py:849
  90.8 0.6 copy-start.11
  91.0 10.1 copy-start.1
  91.8 9.4 copy-start.6
  109.1 125.6 %copy-start.8 = (f32[2,6,1,1024]{3,2,1,0:T(1,128)}, f32[2,6,1,1024]{3,2,1,0:T(1,128)S(1)}, u32[]{:S(2)}) copy-start(f32[2,6,1,1024]{3,2,1,0:T(1,128)S(1)} %reshape.304.bg_ref) | copy-start | bytes 147460
  109.8 331.6 %collective-permute-start.3 = (f32[2,6,1,1024]{3,2,1,0:T(1,128)S(1)}, f32[2,6,1,1024]{3,2,1,0:T(1,128)S(1)}, u32[]{:S(2)}, u32[]{:S(2)}) collective-permute-start(f32[2,6,1,1024]{3,2,1,0:T(1,128)S(1)} %reshape.304.bg_ref), channel_id=1, source_target_pairs={{0,1},{1,0},{2,3},{3,2},{4,5},{5,4},{6,7},{7,6}} | collective-permute-start | bytes 147464 | tf_op jit(solution)/shard_map/ppermute | solution.py:848
  441.4 0.6 copy-start.21
  441.5 0.6 copy-start.19
  803.3 1013.1 %collective-permute-start.7 = (bf16[2,6,2304,1024]{3,2,1,0:T(8,128)(2,1)}, bf16[2,6,2304,1024]{3,2,1,0:T(8,128)(2,1)}, u32[]{:S(2)}, u32[]{:S(2)}) collective-permute-start(bf16[2,6,2304,1024]{3,2,1,0:T(8,128)(2,1)} %get-tuple-element.61), channel_id=1, source_target_pairs={{0,1},{1,0},{2,3},{3,2},{4,5},{5,4},{6,7},{7,6}} | collective-permute-start | bytes 169869312 | tf_op jit(solution)/shard_map/ppermute | solution.py:862
  1256.9 551.2 %reduce-scatter.3.cloned.1.call-start = ((), (), s32[]{:S(2)}) async-start(), calls=%async_computation.4 | async-start | bytes 23592960 | tf_op jit(solution)/shard_map/reduce_scatter | solution.py:868
  1256.9 2.5 copy-start.2
  1257.0 2.6 copy-start.5
  1257.5 788.1 %all-reduce.4.cloned.1.call-start = ((), (), s32[]{:S(2)}) async-start(), calls=%async_computation.6 | async-start | bytes 147456 | tf_op jit(solution)/shard_map/psum | solution.py:883
  1257.5 558.8 %collective-permute-start.8 = (bf16[2,3072,2304]{2,1,0:T(8,128)(2,1)}, bf16[2,3072,2304]{2,1,0:T(8,128)(2,1)}, u32[]{:S(2)}, u32[]{:S(2)}) collective-permute-start(bf16[2,3072,2304]{2,1,0:T(8,128)(2,1)} %get-tuple-element.62), channel_id=1, source_target_pairs={{0,1},{1,0},{2,3},{3,2},{4,5},{5,4},{6,7},{7,6}} | collective-permute-start | bytes 84934664 | tf_op jit(solution)/shard_map/ppermute | solution.py:862
  1257.6 372.9 %collective-permute-start.5 = (bf16[2048,2304]{1,0:T(8,128)(2,1)}, bf16[2048,2304]{1,0:T(8,128)(2,1)}, u32[]{:S(2)}, u32[]{:S(2)}) collective-permute-start(bf16[2048,2304]{1,0:T(8,128)(2,1)} %get-tuple-element.46), channel_id=1, source_target_pairs={{0,4},{4,0},{1,5},{5,1},{2,6},{6,2},{3,7},{7,3}} | collective-permute-start | bytes 28311560 | tf_op jit(solution)/shard_map/ppermute | solution.py:856
  1630.4 15.8 copy-start.22
  1630.4 17.2 copy-start.20
  1630.4 17.2 copy-start.4
  1630.4 17.2 copy-start.14
  1630.4 18.0 copy-start.15
  1630.5 18.6 copy-start.9
  1630.5 23.9 %copy-start.12 = (f32[1024]{0:T(1024)S(1)}, f32[1024]{0:T(1024)}, u32[]{:S(2)}) copy-start(f32[1024]{0:T(1024)} %copy-done.11) | copy-start | bytes 12292
  1646.2 149.2 %collective-permute-start.6 = (bf16[1024,2304]{1,0:T(8,128)(2,1)}, bf16[1024,2304]{1,0:T(8,128)(2,1)}, u32[]{:S(2)}, u32[]{:S(2)}) collective-permute-start(bf16[1024,2304]{1,0:T(8,128)(2,1)} %combine_rows.3), channel_id=1, source_target_pairs={{0,2},{2,0},{1,3},{3,1},{4,6},{6,4},{5,7},{7,5}} | collective-permute-start | bytes 14155784 | tf_op jit(solution)/shard_map/ppermute | solution.py:864
  1646.2 2.2 collective-permute-start.10
  1647.6 1.5 collective-permute-start.9
  1795.4 3.3 copy-start.7
  1795.4 8.0 slice-start
  1798.7 4.8 slice-start.1
Sparse Core Ops, SparseCore 0:
  9.8 171.4 all-gather.3
  183.1 170.9 all-gather.5
  1257.0 46.1 reduce-scatter.4
  1306.7 317.0 reduce-scatter.2
  1771.8 41.5 all-reduce.3

commit v2 on v1

v2 whole, which is shorter than its diff:
```python
import functools
import jax
import jax.numpy as jnp
from jax import lax
from jax.experimental import pallas as pl
from jax.experimental.pallas import tpu as pltpu
from jax.sharding import Mesh, PartitionSpec as P

ZERO = 0
ONE = 1
LANES = 128
LIMIT = 7.0
ALPHA = 1.702
WIN = 256
BLK = 256
FT = 512
GR = 16
F32 = jnp.float32
BF16 = jnp.bfloat16
I32 = jnp.int32
VMEM_MAX = 62 * 1024 * 1024
MT = 3


def params(n_axes):
    return pltpu.CompilerParams(dimension_semantics=('arbitrary',) * n_axes, vmem_limit_bytes=VMEM_MAX)


def dot(lhs, rhs):
    return lax.dot_general(lhs, rhs, (((ONE,), (ZERO,)), ((), ())), preferred_element_type=F32)


def dot_nt(lhs, rhs):
    return lax.dot_general(lhs, rhs, (((ONE,), (ONE,)), ((), ())), preferred_element_type=F32)


def dot_tn(lhs, rhs):
    return lax.dot_general(lhs, rhs, (((ZERO,), (ZERO,)), ((), ())), preferred_element_type=F32)


def mult(value, base):
    return pl.multiple_of(value, base)


class Table:
    def __init__(self, nw):
        self.nw = nw
        self.first, self.count, self.full, self.flat, self.part = (i * 4 * nw for i in range(5))
        base = 20 * nw
        self.end, self.cover, self.mid, self.list0, self.list1 = (base + 4 * i for i in range(5))
        self.seg = base + 20
        self.x = base + 21


def make_table(idx_t, slot_t, x_pos, c_pos, tp_pos, tab):
    tok = idx_t.shape[ONE]
    nw = tab.nw
    nb = tok // LANES
    col = idx_t // 4
    within = idx_t % 4
    local = jnp.where(within // 2 == c_pos, ZERO, 2) + within % 2
    expert = jnp.where((slot_t >= ZERO) & (col == x_pos), local, -ONE)
    ids = jnp.arange(4, dtype=I32)
    hot = jnp.any(expert[:, None, :] == ids[None, :, None], axis=ZERO)
    blocks = hot.astype(BF16).reshape(4, nb, LANES)
    tri = (jnp.arange(LANES)[:, None] <= jnp.arange(LANES)[None, :]).astype(BF16)
    incl = jnp.einsum('ebt,ts->ebs', blocks, tri, preferred_element_type=F32)
    sums = incl[:, :, 127]
    bid = jnp.arange(nb)
    same = (bid[:, None] // (nb // 2)) == (bid[None, :] // (nb // 2))
    before = (same & (bid[:, None] < bid[None, :])).astype(BF16)
    prefix = jnp.einsum('eb,bc->ec', sums.astype(BF16), before, preferred_element_type=F32)
    sums_i = sums.astype(I32)
    prefix_i = prefix.astype(I32)
    n_seg = jnp.sum(sums_i.reshape(4, 2, nb // 2), axis=2)
    pad_seg = (n_seg + GR - ONE) // GR * GR
    mid = pad_seg[:, ZERO]
    base_blk = jnp.where(bid[None, :] >= nb // 2, mid[:, None], ZERO)
    start = base_blk + prefix_i
    wpb = WIN // LANES
    w_start = start.reshape(4, nw, wpb)[:, :, ZERO]
    w_end = w_start + jnp.sum(sums_i.reshape(4, nw, wpb), axis=2)
    first = w_start // GR * GR
    count = ((w_end + GR - ONE) // GR * GR - first) // GR
    wid = jnp.arange(nw)
    last = (wid % (nw // 2)) == nw // 2 - ONE
    full = jnp.where(last[None, :], count, (w_end // GR * GR - first) // GR)
    flat = (jnp.cumsum(count, axis=ZERO) - count) * GR
    part = (w_start % GR != ZERO).astype(I32)
    end = mid + n_seg[:, ONE]
    cover = jnp.maximum((end + 127) // LANES * LANES, LANES)
    lists = (jnp.cumsum(pad_seg, axis=ZERO) - pad_seg)
    row = (start[:, :, None] + incl.astype(I32) - ONE).reshape(4, nw, WIN)
    flat_row = (row - first[:, :, None] + flat[:, :, None]).reshape(4, tok)
    pos = jnp.max(jnp.where(expert[:, None, :] == ids[None, :, None], flat_row[None], -ONE), axis=ONE)
    vec = jnp.concatenate([
        first.reshape(-ONE), count.reshape(-ONE), full.reshape(-ONE), flat.reshape(-ONE), part.reshape(-ONE),
        end, cover, mid, lists[:, ZERO], lists[:, ONE], jnp.stack([tp_pos, x_pos]).astype(I32)])
    return vec.astype(I32), pos.astype(I32)


def pair_matrix():
    i = lax.broadcasted_iota(I32, (256, 256), ZERO)
    n = lax.broadcasted_iota(I32, (256, 256), ONE)
    src = jnp.where(n < LANES, 2 * n, 2 * n - 255)
    return jnp.where(i == src, 1.0, 0.0).astype(BF16)


def pair_matrix_t():
    i = lax.broadcasted_iota(I32, (256, 256), ONE)
    n = lax.broadcasted_iota(I32, (256, 256), ZERO)
    src = jnp.where(n < LANES, 2 * n, 2 * n - 255)
    return jnp.where(i == src, 1.0, 0.0).astype(BF16)


def split_weights(w_gu):
    n_e, dim, width = w_gu.shape
    nf = pl.cdiv(width, 2 * FT)
    rows = dim // MT

    def body(w_ref, o_ref):
        f = pl.program_id(ONE)
        mat = pair_matrix()

        def go(valid):
            for g in range(2 * FT // 256):
                lo, hi = 256 * g, min(256 * g + 256, valid)
                if hi > lo:
                    res = dot(w_ref[ZERO, :, lo:hi], mat[:hi - lo]).astype(BF16)
                else:
                    res = jnp.zeros((rows, 256), BF16)
                o_ref[ZERO, ZERO, :, LANES * g:LANES * g + LANES] = res[:, :LANES]
                o_ref[ZERO, ZERO, :, FT + LANES * g:FT + LANES * g + LANES] = res[:, LANES:]

        @pl.when(f < nf - ONE)
        def _():
            go(2 * FT)

        @pl.when(f == nf - ONE)
        def _():
            go(width - (nf - ONE) * 2 * FT)

    return pl.pallas_call(
        body, name='split_weights', grid=(n_e, nf, MT),
        in_specs=[pl.BlockSpec((ONE, rows, 2 * FT), lambda e, f, r: (e, r, f))],
        out_specs=pl.BlockSpec((ONE, ONE, rows, 2 * FT), lambda e, f, r: (e, f, r, ZERO)),
        out_shape=jax.ShapeDtypeStruct((n_e, nf, dim, 2 * FT), BF16),
        compiler_params=params(3),
        cost_estimate=pl.CostEstimate(flops=2 * n_e * dim * width * 256, bytes_accessed=4 * n_e * dim * width, transcendentals=ZERO),
    )(w_gu)


def flat_blocks(tab_ref, tab, w):
    rows = tab_ref[tab.flat + 3 * tab.nw + w] + GR * tab_ref[tab.count + 3 * tab.nw + w]
    return (rows + BLK - ONE) // BLK


FLAT = 3 * BLK


def gather_rows(vec, pos, tokens, cap, tab, wk=None):
    tok, dim = tokens.shape
    nw = tab.nw

    def body(tab_ref, *refs):
        if wk is None:
            pos_ref, x_ref, *out_refs, fb, carry, zero, sem, zsem = refs
        else:
            pos_ref, wk_ref, x_ref, *out_refs, fb, carry, zero, sem, zsem = refs
        w = pl.program_id(ZERO)
        slot = lax.rem(w, 2)

        def drain(win, which):
            n = sum(tab_ref[tab.full + e * nw + win] for e in range(4))

            def one(_, c):
                pltpu.make_async_copy(fb.at[ZERO, pl.ds(ZERO, GR)], out_refs[ZERO].at[ZERO, pl.ds(ZERO, GR)], sem.at[which]).wait()
                return c

            lax.fori_loop(ZERO, n, one, ZERO)

        @pl.when(w == ZERO)
        def _():
            zero[...] = jnp.zeros_like(zero)

        @pl.when(w >= 2)
        def _():
            drain(w - 2, slot)

        def block(b, c):
            j = lax.broadcasted_iota(I32, (BLK, WIN), ZERO) + b * BLK
            m0 = pos_ref[ZERO:ONE, :] == j
            m1 = pos_ref[ONE:2, :] == j
            hot = jnp.where(m0 | m1, 1.0, 0.0).astype(BF16)
            res = dot(hot, x_ref[...])
            if wk is not None:
                scale = jnp.where(m0, wk_ref[ZERO:ONE, :], 0.0) + jnp.where(m1, wk_ref[ONE:2, :], 0.0)
                res = res * jnp.sum(scale, axis=ONE, keepdims=True)
            fb[slot, pl.ds(mult(b * BLK, BLK), BLK), :] = res.astype(BF16)
            return c

        lax.fori_loop(ZERO, flat_blocks(tab_ref, tab, w), block, ZERO)

        for e in range(4):
            at = e * nw + w
            n_groups = tab_ref[tab.count + at]
            off = tab_ref[tab.flat + at]
            first = tab_ref[tab.first + at]

            @pl.when(n_groups > ZERO)
            def _():
                head = pl.ds(mult(off, GR), GR)

                @pl.when(tab_ref[tab.part + at] == ONE)
                def _():
                    fb[slot, head, :] = fb[slot, head, :] + carry[e]

                carry[e] = fb[slot, pl.ds(mult(off + GR * (n_groups - ONE), GR), GR), :]

            def send(g, c):
                pltpu.make_async_copy(
                    fb.at[slot, pl.ds(mult(off + GR * g, GR), GR)],
                    out_refs[e // 2].at[e % 2, pl.ds(mult(first + GR * g, GR), GR)], sem.at[slot]).start()
                return c

            lax.fori_loop(ZERO, tab_ref[tab.full + at], send, ZERO)

        @pl.when(w == nw - ONE)
        def _():
            for e in range(4):
                lo = (tab_ref[tab.end + e] + GR - ONE) // GR
                hi = tab_ref[tab.cover + e] // GR

                def fill(g, c):
                    pltpu.make_async_copy(zero, out_refs[e // 2].at[e % 2, pl.ds(mult(g * GR, GR), GR)], zsem).start()
                    return c

                lax.fori_loop(lo, hi, fill, ZERO)

                def done(g, c):
                    pltpu.make_async_copy(zero, out_refs[ZERO].at[ZERO, pl.ds(ZERO, GR)], zsem).wait()
                    return c

                lax.fori_loop(lo, hi, done, ZERO)
            drain(w - ONE, ONE - slot)
            drain(w, slot)

    args = [vec, pos] + ([] if wk is None else [wk]) + [tokens]
    small = pl.BlockSpec((2, WIN), lambda w, t: (ZERO, w))
    return pl.pallas_call(
        body, name='gather_rows',
        grid_spec=pltpu.PrefetchScalarGridSpec(
            num_scalar_prefetch=ONE, grid=(nw,),
            in_specs=[small] * (len(args) - 2) + [pl.BlockSpec((WIN, dim), lambda w, t: (w, ZERO))],
            out_specs=[pl.BlockSpec(memory_space=pl.ANY)] * 2,
            scratch_shapes=[pltpu.VMEM((2, FLAT, dim), BF16), pltpu.VMEM((4, GR, dim), BF16), pltpu.VMEM((GR, dim), BF16),
                            pltpu.SemaphoreType.DMA((2,)), pltpu.SemaphoreType.DMA]),
        out_shape=[jax.ShapeDtypeStruct((2, cap, dim), BF16)] * 2,
        compiler_params=params(ONE),
        cost_estimate=pl.CostEstimate(flops=8 * tok * 256 * dim, bytes_accessed=4 * tok * dim, transcendentals=ZERO),
    )(*args)


def swiglu_parts(h):
    gate, up = h[:, :FT], h[:, FT:]
    g = jnp.minimum(gate, LIMIT)
    u1 = jnp.clip(up, -LIMIT, LIMIT) + 1.0
    s = jax.nn.sigmoid(ALPHA * g)
    return gate, up, g, u1, s


def stages(tail, per_tile, n_tiles, stage):
    total = per_tile * n_tiles

    def size(t):
        return jnp.where((lax.rem(t, per_tile) == per_tile - ONE) & tail, LANES, BLK)

    def step(t, c):
        prev = jnp.where(t > ZERO, size(t - ONE), ZERO)
        nxt = jnp.where(t < total, size(t), ZERO)
        for pm in (ZERO, LANES, BLK):
            for nm in (ZERO, LANES, BLK):
                if pm or nm:
                    @pl.when((prev == pm) & (nxt == nm))
                    def _():
                        stage(t, pm, nm)
        return c

    lax.fori_loop(ZERO, total + ONE, step, ZERO)


class Feed:
    def __init__(self, tab_ref, tab, rows_own, rows_oth, row_buf, row_sem, wg_own, wg_oth, wd_own, wd_oth, wg_buf, wd_buf, w_sem):
        self.tab_ref, self.tab = tab_ref, tab
        self.rows, self.row_buf, self.row_sem = (rows_own, rows_oth), row_buf, row_sem
        self.wg, self.wd = (wg_own, wg_oth), (wd_own, wd_oth)
        self.wg_buf, self.wd_buf, self.w_sem = wg_buf, wd_buf, w_sem

    def _row_copies(self, e, go):
        slot = lax.rem(e, 2)
        for half in range(2):
            @pl.when(e // 2 == half)
            def _():
                def one(k, c):
                    at = pl.ds(mult(k * LANES, LANES), LANES)
                    go(pltpu.make_async_copy(self.rows[half].at[slot, at], self.row_buf.at[slot, at], self.row_sem.at[slot]))
                    return c

                lax.fori_loop(ZERO, self.tab_ref[self.tab.cover + e] // LANES, one, ZERO)

    def start_rows(self, e):
        self._row_copies(e, lambda d: d.start())

    def wait_rows(self, e):
        self._row_copies(e, lambda d: d.wait())

    def _tile_copies(self, e, f, slot, go):
        for half in range(2):
            @pl.when(e // 2 == half)
            def _():
                k = lax.rem(e, 2)
                go(pltpu.make_async_copy(self.wg[half].at[k, f], self.wg_buf.at[slot], self.w_sem.at[slot]))
                go(pltpu.make_async_copy(self.wd[half].at[k, pl.ds(mult(f * FT, FT), FT)], self.wd_buf.at[slot], self.w_sem.at[2 + slot]))

    def start_tile(self, e, f, slot):
        self._tile_copies(e, f, slot, lambda d: d.start())

    def wait_tile(self, e, f, slot):
        self._tile_copies(e, f, slot, lambda d: d.wait())


def expert_forward(vec, x_rows, wg, wd, bg, bd, main_rows, tab):
    half_e, nf, dim, _ = wg[ZERO].shape
    n_e = 2 * half_e
    cap = x_rows[ZERO].shape[ONE]
    list_rows = 2 * cap + 4 * GR

    def body(tab_ref, xo, xt, go, gt, do, dt, bg_ref, bd_ref, h_ref, ao_ref, at_ref, keep_ref, main_ref, over_ref,
             x_buf, x_sem, wg_buf, wd_buf, w_sem, acc, h_now, h_st, a_st, p_st, pend, o_sem, p_sem):
        e = pl.program_id(ZERO)
        feed = Feed(tab_ref, tab, xo, xt, x_buf, x_sem, go, gt, do, dt, wg_buf, wd_buf, w_sem)
        cover = tab_ref[tab.cover + e]
        n_full = cover // BLK
        tail = cover % BLK != ZERO
        per_tile = n_full + tail.astype(I32)
        xs = lax.rem(e, 2)

        @pl.when(e == ZERO)
        def _():
            for i in range(4):
                pend[i] = ZERO
            feed.start_rows(ZERO)
            feed.start_tile(ZERO, ZERO, ZERO)

        @pl.when(e + ONE < n_e)
        def _():
            feed.start_rows(e + ONE)

        feed.wait_rows(e)

        def wait_p(slot):
            def one(_, c):
                pltpu.make_async_copy(p_st.at[ZERO, pl.ds(ZERO, GR)], keep_ref.at[pl.ds(ZERO, GR)], p_sem.at[slot]).wait()
                return c

            lax.fori_loop(ZERO, pend[2 + slot], one, ZERO)
            pend[2 + slot] = ZERO

        def wait_out(slot):
            @pl.when(pend[slot] == ONE)
            def _():
                pltpu.make_async_copy(h_st.at[ZERO], h_ref.at[ZERO, pl.ds(ZERO, BLK), pl.ds(ZERO, 2 * FT)], o_sem.at[slot]).wait()
                pltpu.make_async_copy(a_st.at[ZERO], ao_ref.at[ZERO, pl.ds(ZERO, BLK), pl.ds(ZERO, FT)], o_sem.at[2 + slot]).wait()
                pend[slot] = ZERO

        def stage(t, pm, nm):
            tp = jnp.maximum(t - ONE, ZERO)
            fp, fn = tp // per_tile, t // per_tile
            ip, ix = tp - fp * per_tile, t - fn * per_tile
            sp, sn = lax.rem(e * nf + fp, 2), lax.rem(e * nf + fn, 2)
            slot = lax.rem(tp, 2)
            if pm:
                wait_out(slot)
            if nm:
                @pl.when(ix == ZERO)
                def _():
                    feed.wait_tile(e, fn, sn)
            rp = mult(ip * BLK, BLK)
            if pm:
                h = h_now[:pm]
                h_st[slot, :pm] = h
                _, _, g, u1, s = swiglu_parts(h)
                a = (g * s * u1).astype(BF16)
                a_st[slot, :pm] = a
            if nm:
                h_now[:nm] = dot(x_buf[xs, pl.ds(mult(ix * BLK, BLK), nm), :], wg_buf[sn]) + bg_ref[ZERO, fn]
            if pm:
                part = dot(a, wd_buf[sp])
                rows = pl.ds(rp, pm)
                acc[rows, :] = part + jnp.where(fp == ZERO, 0.0, acc[rows, :])
                to_h = h_ref.at[e, pl.ds(rp, BLK), pl.ds(mult(fp * 2 * FT, 2 * FT), 2 * FT)]
                pltpu.make_async_copy(h_st.at[slot], to_h, o_sem.at[slot]).start()
                for half, ref in ((ZERO, ao_ref), (ONE, at_ref)):
                    @pl.when(e // 2 == half)
                    def _():
                        to_a = ref.at[xs, pl.ds(rp, BLK), pl.ds(mult(fp * FT, FT), FT)]
                        pltpu.make_async_copy(a_st.at[slot], to_a, o_sem.at[2 + slot]).start()
                pend[slot] = ONE
            if nm:
                at = e * nf + fn + ONE

                @pl.when((ix == ZERO) & (at < n_e * nf))
                def _():
                    feed.start_tile(at // nf, lax.rem(at, nf), lax.rem(at, 2))

        stages(tail, per_tile, nf, stage)

        end = tab_ref[tab.end + e]
        mid = tab_ref[tab.mid + e]
        seg = tab_ref[tab.seg]

        def put(i, c):
            r0 = mult(i * LANES, LANES)
            slot = lax.rem(i, 2)
            wait_p(slot)
            p_st[slot] = (acc[pl.ds(r0, LANES), :] + bd_ref[ZERO]).astype(BF16)
            n = jnp.clip((end - r0 + GR - ONE) // GR, ZERO, LANES // GR)

            def send(k, c2):
                r = r0 + k * GR
                in1 = (r >= mid).astype(I32)
                to = jnp.where(in1 == ONE, tab_ref[tab.list1 + e] + r - mid, tab_ref[tab.list0 + e] + r)
                src = p_st.at[slot, pl.ds(mult(k * GR, GR), GR)]

                @pl.when(in1 == seg)
                def _():
                    pltpu.make_async_copy(src, keep_ref.at[pl.ds(mult(to, GR), GR)], p_sem.at[slot]).start()

                @pl.when((in1 != seg) & (to < main_rows))
                def _():
                    pltpu.make_async_copy(src, main_ref.at[pl.ds(mult(to, GR), GR)], p_sem.at[slot]).start()

                @pl.when((in1 != seg) & (to >= main_rows))
                def _():
                    pltpu.make_async_copy(src, over_ref.at[pl.ds(mult(to - main_rows, GR), GR)], p_sem.at[slot]).start()

                return c2

            lax.fori_loop(ZERO, n, send, ZERO)
            pend[2 + slot] = n
            return c

        lax.fori_loop(ZERO, cover // LANES, put, ZERO)

        @pl.when(e == n_e - ONE)
        def _():
            for slot in range(2):
                wait_out(slot)
                wait_p(slot)

    any_spec = pl.BlockSpec(memory_space=pl.ANY)
    dma2 = pltpu.SemaphoreType.DMA((2,))
    dma4 = pltpu.SemaphoreType.DMA((4,))
    act = jax.ShapeDtypeStruct((half_e, cap, nf * FT), BF16)
    return pl.pallas_call(
        body, name='expert_forward',
        grid_spec=pltpu.PrefetchScalarGridSpec(
            num_scalar_prefetch=ONE, grid=(n_e,),
            in_specs=[any_spec] * 6 + [pl.BlockSpec((ONE, nf, ONE, 2 * FT), lambda e, t: (e, ZERO, ZERO, ZERO)), pl.BlockSpec((ONE, ONE, dim), lambda e, t: (e, ZERO, ZERO))],
            out_specs=[any_spec] * 6,
            scratch_shapes=[pltpu.VMEM((2, cap, dim), BF16), dma2, pltpu.VMEM((2, dim, 2 * FT), BF16), pltpu.VMEM((2, FT, dim), BF16), dma4,
                            pltpu.VMEM((cap, dim), F32), pltpu.VMEM((BLK, 2 * FT), F32), pltpu.VMEM((2, BLK, 2 * FT), F32),
                            pltpu.VMEM((2, BLK, FT), BF16), pltpu.VMEM((2, LANES, dim), BF16), pltpu.SMEM((4,), I32), dma4, dma2]),
        out_shape=[jax.ShapeDtypeStruct((n_e, cap, nf * 2 * FT), F32), act, act, jax.ShapeDtypeStruct((list_rows, dim), BF16),
                   jax.ShapeDtypeStruct((main_rows, dim), BF16), jax.ShapeDtypeStruct((list_rows - main_rows, dim), BF16)],
        compiler_params=params(ONE),
        cost_estimate=pl.CostEstimate(flops=6 * n_e * 1024 * dim * nf * FT, bytes_accessed=n_e * nf * dim * FT * 6, transcendentals=ZERO),
    )(vec, *x_rows, *wg, *wd, bg, bd)


def expert_backward(vec, d_rows, wg, wd, bd, h_all, tab):
    half_e, nf, dim, _ = wg[ZERO].shape
    n_e = 2 * half_e
    cap = d_rows[ZERO].shape[ONE]

    def body(tab_ref, do_in, dt_in, go, gt, do, dt, bd_ref, h_ref, dho_ref, dht_ref, dx_ref, g_ref, sbg_ref, sbd_ref,
             d_buf, d_sem, wg_buf, wd_buf, w_sem, acc, gacc, da_now, h_buf, dh_st, dx_st, g_st, pend, h_sem, o_sem, x_sem):
        e = pl.program_id(ZERO)
        feed = Feed(tab_ref, tab, do_in, dt_in, d_buf, d_sem, go, gt, do, dt, wg_buf, wd_buf, w_sem)
        cover = tab_ref[tab.cover + e]
        n_full = cover // BLK
        tail = cover % BLK != ZERO
        per_tile = n_full + tail.astype(I32)
        ds = lax.rem(e, 2)

        @pl.when(e == ZERO)
        def _():
            for i in range(4):
                pend[i] = ZERO
            feed.start_rows(ZERO)
            feed.start_tile(ZERO, ZERO, ZERO)

        @pl.when(e + ONE < n_e)
        def _():
            feed.start_rows(e + ONE)

        def load(t):
            ff = t // per_tile
            src = h_ref.at[e, pl.ds(mult((t - ff * per_tile) * BLK, BLK), BLK), pl.ds(mult(ff * 2 * FT, 2 * FT), 2 * FT)]
            return pltpu.make_async_copy(src, h_buf.at[lax.rem(t, 2)], h_sem.at[lax.rem(t, 2)])

        load(ZERO).start()
        feed.wait_rows(e)
        sbg_ref[...] = jnp.zeros_like(sbg_ref)

        def wait_dh(slot):
            @pl.when(pend[slot] == ONE)
            def _():
                pltpu.make_async_copy(dh_st.at[ZERO], dho_ref.at[ZERO, pl.ds(ZERO, BLK), pl.ds(ZERO, 2 * FT)], o_sem.at[slot]).wait()
                pend[slot] = ZERO

        def wait_dx(slot):
            @pl.when(pend[2 + slot] == ONE)
            def _():
                pltpu.make_async_copy(dx_st.at[ZERO], dx_ref.at[ZERO, pl.ds(ZERO, LANES)], x_sem.at[slot]).wait()
                pltpu.make_async_copy(g_st.at[ZERO], g_ref.at[ZERO, pl.ds(ZERO, LANES)], x_sem.at[2 + slot]).wait()
                pend[2 + slot] = ZERO

        def stage(t, pm, nm):
            tp = jnp.maximum(t - ONE, ZERO)
            fp, fn = tp // per_tile, t // per_tile
            ip, ix = tp - fp * per_tile, t - fn * per_tile
            sp, sn = lax.rem(e * nf + fp, 2), lax.rem(e * nf + fn, 2)
            slot = lax.rem(tp, 2)
            if pm:
                wait_dh(slot)
                load(tp).wait()
            if nm:
                @pl.when(t > ZERO)
                def _():
                    load(t).start()

                @pl.when(ix == ZERO)
                def _():
                    feed.wait_tile(e, fn, sn)
            rp = mult(ip * BLK, BLK)
            rows = pl.ds(rp, pm)
            if pm:
                da = da_now[:pm]
                gate, up, g, u1, s = swiglu_parts(h_buf[slot, :pm])
                gs = g * s
                a = (gs * u1).astype(BF16).astype(F32)
                pass_g = jnp.where(gate < LIMIT, 1.0, jnp.where(gate == LIMIT, 0.5, 0.0))
                pass_u = jnp.where(jnp.abs(up) < LIMIT, 1.0, jnp.where(jnp.abs(up) == LIMIT, 0.5, 0.0))
                dg = da * pass_g * (u1 * (s + ALPHA * gs * (1.0 - s)))
                du = da * pass_u * gs
                sbg_ref[ZERO, fp, :, :FT] += jnp.sum(dg, axis=ZERO, keepdims=True)
                sbg_ref[ZERO, fp, :, FT:] += jnp.sum(du, axis=ZERO, keepdims=True)
                prod = a * da
                gpart = sum(prod[:, LANES * q:LANES * q + LANES] for q in range(FT // LANES))
                gacc[rows, :] = gpart + jnp.where(fp == ZERO, 0.0, gacc[rows, :])
                dh = jnp.concatenate([dg.astype(BF16), du.astype(BF16)], axis=ONE)
                dh_st[slot, :pm] = dh
            if nm:
                da_now[:nm] = dot_nt(d_buf[ds, pl.ds(mult(ix * BLK, BLK), nm), :], wd_buf[sn])
            if pm:
                part = dot_nt(dh, wg_buf[sp])
                acc[rows, :] = part + jnp.where(fp == ZERO, 0.0, acc[rows, :])
                for half, ref in ((ZERO, dho_ref), (ONE, dht_ref)):
                    @pl.when(e // 2 == half)
                    def _():
                        to = ref.at[ds, pl.ds(rp, BLK), pl.ds(mult(fp * 2 * FT, 2 * FT), 2 * FT)]
                        pltpu.make_async_copy(dh_st.at[slot], to, o_sem.at[slot]).start()
                pend[slot] = ONE
            if nm:
                at = e * nf + fn + ONE

                @pl.when((ix == ZERO) & (at < n_e * nf))
                def _():
                    feed.start_tile(at // nf, lax.rem(at, nf), lax.rem(at, 2))

        stages(tail, per_tile, nf, stage)

        sbd_ref[...] = jnp.zeros_like(sbd_ref)

        def put(i, c):
            rows = pl.ds(mult(i * LANES, LANES), LANES)
            slot = lax.rem(i, 2)
            wait_dx(slot)
            dx_st[slot] = acc[rows, :].astype(BF16)
            d32 = d_buf[ds, rows, :].astype(F32)
            sbd_ref[ZERO] += jnp.sum(d32, axis=ZERO, keepdims=True)
            db = d32 * bd_ref[ZERO]
            total = jnp.sum(gacc[rows, :] + sum(db[:, LANES * q:LANES * q + LANES] for q in range(dim // LANES)), axis=ONE, keepdims=True)
            hi = total.astype(BF16).astype(F32)
            rest = total - hi
            mid = rest.astype(BF16).astype(F32)
            lane = lax.broadcasted_iota(I32, (LANES, LANES), ONE)
            g_st[slot] = jnp.where(lane == ZERO, hi, jnp.where(lane == ONE, mid, jnp.where(lane == 2, rest - mid, 0.0))).astype(BF16)
            pltpu.make_async_copy(dx_st.at[slot], dx_ref.at[e, rows], x_sem.at[slot]).start()
            pltpu.make_async_copy(g_st.at[slot], g_ref.at[e, rows], x_sem.at[2 + slot]).start()
            pend[2 + slot] = ONE
            return c

        lax.fori_loop(ZERO, cover // LANES, put, ZERO)

        @pl.when(e == n_e - ONE)
        def _():
            for slot in range(2):
                wait_dh(slot)
                wait_dx(slot)

    any_spec = pl.BlockSpec(memory_space=pl.ANY)
    dma2 = pltpu.SemaphoreType.DMA((2,))
    dma4 = pltpu.SemaphoreType.DMA((4,))
    dh_shape = jax.ShapeDtypeStruct((half_e, cap, nf * 2 * FT), BF16)
    return pl.pallas_call(
        body, name='expert_backward',
        grid_spec=pltpu.PrefetchScalarGridSpec(
            num_scalar_prefetch=ONE, grid=(n_e,),
            in_specs=[any_spec] * 6 + [pl.BlockSpec((ONE, ONE, dim), lambda e, t: (e, ZERO, ZERO)), any_spec],
            out_specs=[any_spec] * 4 + [pl.BlockSpec((ONE, nf, ONE, 2 * FT), lambda e, t: (e, ZERO, ZERO, ZERO)), pl.BlockSpec((ONE, ONE, dim), lambda e, t: (e, ZERO, ZERO))],
            scratch_shapes=[pltpu.VMEM((2, cap, dim), BF16), dma2, pltpu.VMEM((2, dim, 2 * FT), BF16), pltpu.VMEM((2, FT, dim), BF16), dma4,
                            pltpu.VMEM((cap, dim), F32), pltpu.VMEM((cap, LANES), F32), pltpu.VMEM((BLK, FT), F32),
                            pltpu.VMEM((2, BLK, 2 * FT), F32), pltpu.VMEM((2, BLK, 2 * FT), BF16), pltpu.VMEM((2, LANES, dim), BF16),
                            pltpu.VMEM((2, LANES, LANES), BF16), pltpu.SMEM((4,), I32), dma2, dma2, dma4]),
        out_shape=[dh_shape, dh_shape, jax.ShapeDtypeStruct((n_e, cap, dim), BF16), jax.ShapeDtypeStruct((n_e, cap, LANES), BF16),
                   jax.ShapeDtypeStruct((n_e, nf, ONE, 2 * FT), F32), jax.ShapeDtypeStruct((n_e, ONE, dim), F32)],
        compiler_params=params(ONE),
        cost_estimate=pl.CostEstimate(flops=6 * n_e * 1024 * dim * nf * FT, bytes_accessed=n_e * nf * dim * FT * 6, transcendentals=ZERO),
    )(vec, *d_rows, *wg, *wd, bd, h_all)


CHUNK = 512


def weight_grads(vecs, x_rows, d_rows, dh, a, tab, width):
    n_e, cap, wide = dh[ZERO].shape
    dim = x_rows[ZERO].shape[2]
    nf = wide // (2 * FT)
    mrows = dim // MT
    piece = LANES

    def body(tab0, tab1, x0, x1, d0, d1, h0, h1, a0, a1, og_ref, od_ref, x_t, x_st, h_buf, a_buf, d_buf, a_t, acc_g, acc_d, x_sem, sem):
        e = pl.program_id(ZERO)
        f = pl.program_id(ONE)

        def counts(ee):
            first = tab0[tab.cover + ee] // piece
            return first, first + tab1[tab.cover + 2 + ee] // piece

        n0, n_all = counts(e)
        n_chunks = (n_all * piece + CHUNK - ONE) // CHUNK

        def pieces(ee, ff, chunk, slot, go):
            lo, hi = counts(ee)

            def one(k, c):
                v = chunk * (CHUNK // piece) + k
                to = pl.ds(mult(k * piece, piece), piece)
                for cond, xd, xh, xa, at in ((v < lo, d0, h0, a0, v), (v >= lo, d1, h1, a1, v - lo)):
                    @pl.when(cond)
                    def _():
                        src = pl.ds(mult(at * piece, piece), piece)
                        go(pltpu.make_async_copy(xh.at[ee, src, pl.ds(mult(ff * 2 * FT, 2 * FT), 2 * FT)], h_buf.at[slot, to], sem.at[slot]))
                        go(pltpu.make_async_copy(xa.at[ee, src, pl.ds(mult(ff * FT, FT), FT)], a_buf.at[slot, to], sem.at[2 + slot]))
                        go(pltpu.make_async_copy(xd.at[ee, src], d_buf.at[slot, to], sem.at[4 + slot]))
                return c

            lax.fori_loop(ZERO, jnp.minimum(CHUNK // piece, hi - chunk * (CHUNK // piece)), one, ZERO)

        def x_copy(v, go):
            for cond, ref, at in ((v < n0, x0, v), (v >= n0, x1, v - n0)):
                @pl.when(cond)
                def _():
                    go(pltpu.make_async_copy(ref.at[e, pl.ds(mult(at * piece, piece), piece)], x_st.at[lax.rem(v, 2)], x_sem.at[lax.rem(v, 2)]))

        @pl.when((e == ZERO) & (f == ZERO))
        def _():
            pieces(ZERO, ZERO, ZERO, ZERO, lambda c: c.start())

        @pl.when(f == ZERO)
        def _():
            x_copy(ZERO, lambda c: c.start())

            def turn(v, c):
                @pl.when(v + ONE < n_all)
                def _():
                    x_copy(v + ONE, lambda d: d.start())

                x_copy(v, lambda d: d.wait())
                x_t[:, pl.ds(mult(v * piece, piece), piece)] = x_st[lax.rem(v, 2)].T
                return c

            lax.fori_loop(ZERO, n_all, turn, ZERO)

        def work(chunk, slot, size):
            a_t[:, :size] = a_buf[slot, :size, :].T

            def part(m, c):
                cols = pl.ds(mult(m * mrows, LANES), mrows)
                xs = x_t[cols, pl.ds(mult(chunk * CHUNK, LANES), size)]
                acc_g[cols, :] = dot(xs, h_buf[slot, :size, :]) + jnp.where(chunk == ZERO, 0.0, acc_g[cols, :])
                acc_d[:, cols] = dot(a_t[:, :size], d_buf[slot, :size, cols]) + jnp.where(chunk == ZERO, 0.0, acc_d[:, cols])
                return c

            lax.fori_loop(ZERO, MT, part, ZERO)

        def total_before(ee):
            _, hi = counts(ZERO)
            return jnp.where(ee > ZERO, nf * ((hi * piece + CHUNK - ONE) // CHUNK), ZERO)

        def loop(chunk, c):
            count = total_before(e) + f * n_chunks + chunk
            slot = lax.rem(count, 2)
            more = chunk + ONE < n_chunks
            next_f = f + ONE < nf

            @pl.when(more)
            def _():
                pieces(e, f, chunk + ONE, ONE - slot, lambda d: d.start())

            @pl.when(jnp.logical_not(more) & (next_f | (e + ONE < n_e)))
            def _():
                pieces(jnp.where(next_f, e, e + ONE), jnp.where(next_f, f + ONE, ZERO), ZERO, ONE - slot, lambda d: d.start())

            pieces(e, f, chunk, slot, lambda d: d.wait())
            rows = n_all * piece - chunk * CHUNK

            @pl.when(rows >= CHUNK)
            def _():
                work(chunk, slot, CHUNK)

            for size in range(LANES, CHUNK, LANES):
                @pl.when(rows == size)
                def _():
                    work(chunk, slot, size)
            return c

        lax.fori_loop(ZERO, n_chunks, loop, ZERO)

        od_ref[ZERO] = acc_d[...].astype(BF16)
        mat = pair_matrix_t()

        def flush(m, c):
            cols = pl.ds(mult(m * mrows, LANES), mrows)
            for g in range(2 * FT // 256):
                pair = jnp.concatenate([acc_g[cols, LANES * g:LANES * g + LANES].astype(BF16), acc_g[cols, FT + LANES * g:FT + LANES * g + LANES].astype(BF16)], axis=ONE)
                og_ref[ZERO, cols, 256 * g:256 * g + 256] = dot(pair, mat).astype(BF16)
            return c

        lax.fori_loop(ZERO, MT, flush, ZERO)

    any_spec = pl.BlockSpec(memory_space=pl.ANY)
    return pl.pallas_call(
        body, name='weight_grads',
        grid_spec=pltpu.PrefetchScalarGridSpec(
            num_scalar_prefetch=2, grid=(n_e, nf),
            in_specs=[any_spec] * 8,
            out_specs=[pl.BlockSpec((ONE, dim, 2 * FT), lambda e, f, *t: (e, ZERO, f)), pl.BlockSpec((ONE, FT, dim), lambda e, f, *t: (e, f, ZERO))],
            scratch_shapes=[pltpu.VMEM((dim, 2 * cap), BF16), pltpu.VMEM((2, piece, dim), BF16), pltpu.VMEM((2, CHUNK, 2 * FT), BF16),
                            pltpu.VMEM((2, CHUNK, FT), BF16), pltpu.VMEM((2, CHUNK, dim), BF16), pltpu.VMEM((FT, CHUNK), BF16),
                            pltpu.VMEM((dim, 2 * FT), F32), pltpu.VMEM((FT, dim), F32), pltpu.SemaphoreType.DMA((2,)), pltpu.SemaphoreType.DMA((6,))]),
        out_shape=[jax.ShapeDtypeStruct((n_e, dim, width), BF16), jax.ShapeDtypeStruct((n_e, width // 2, dim), BF16)],
        compiler_params=params(2),
        cost_estimate=pl.CostEstimate(flops=12 * n_e * 1024 * dim * nf * FT, bytes_accessed=n_e * nf * dim * FT * 6, transcendentals=ZERO),
    )(*vecs, *x_rows, *d_rows, *dh, *a)


def scatter_rows(vec, pos, dx_rows, g_rows, tok, tab):
    dim = dx_rows.shape[2]
    nw = tab.nw

    def body(tab_ref, pos_ref, x_ref, g_ref, out_ref, gout_ref, fb, gb, acc, gacc, sem):
        w = pl.program_id(ZERO)
        slot = lax.rem(w, 2)

        def fetch(win, to):
            for e in range(4):
                at = e * nw + win

                def one(k, c):
                    rows = pl.ds(mult(tab_ref[tab.first + at] + GR * k, GR), GR)
                    put = pl.ds(mult(tab_ref[tab.flat + at] + GR * k, GR), GR)
                    pltpu.make_async_copy(x_ref.at[e, rows], fb.at[to, put], sem.at[to]).start()
                    pltpu.make_async_copy(g_ref.at[e, rows], gb.at[to, put], sem.at[2 + to]).start()
                    return c

                lax.fori_loop(ZERO, tab_ref[tab.count + at], one, ZERO)

        @pl.when(w == ZERO)
        def _():
            fb[...] = jnp.zeros_like(fb)
            gb[...] = jnp.zeros_like(gb)
            fetch(ZERO, ZERO)

        @pl.when(w + ONE < nw)
        def _():
            fetch(w + ONE, ONE - slot)

        def one_wait(k, c):
            pltpu.make_async_copy(x_ref.at[ZERO, pl.ds(ZERO, GR)], fb.at[slot, pl.ds(ZERO, GR)], sem.at[slot]).wait()
            pltpu.make_async_copy(g_ref.at[ZERO, pl.ds(ZERO, GR)], gb.at[slot, pl.ds(ZERO, GR)], sem.at[2 + slot]).wait()
            return c

        lax.fori_loop(ZERO, sum(tab_ref[tab.count + e * nw + w] for e in range(4)), one_wait, ZERO)

        acc[...] = jnp.zeros_like(acc)
        gacc[...] = jnp.zeros_like(gacc)

        def block(b, c):
            j = lax.broadcasted_iota(I32, (BLK, WIN), ZERO) + b * BLK
            m0 = pos_ref[ZERO:ONE, :] == j
            m1 = pos_ref[ONE:2, :] == j
            rows = pl.ds(mult(b * BLK, BLK), BLK)
            acc[...] += dot_tn(jnp.where(m0 | m1, 1.0, 0.0).astype(BF16), fb[slot, rows, :])
            gv = gb[slot, rows, :]
            gacc[ZERO] += dot_tn(jnp.where(m0, 1.0, 0.0).astype(BF16), gv)
            gacc[ONE] += dot_tn(jnp.where(m1, 1.0, 0.0).astype(BF16), gv)
            return c

        lax.fori_loop(ZERO, flat_blocks(tab_ref, tab, w), block, ZERO)
        out_ref[...] = acc[...].astype(BF16)
        lane = lax.broadcasted_iota(I32, (WIN, LANES), ONE)
        g0 = jnp.sum(gacc[ZERO], axis=ONE, keepdims=True)
        g1 = jnp.sum(gacc[ONE], axis=ONE, keepdims=True)
        gout_ref[...] = jnp.where(lane == ZERO, g0, jnp.where(lane == ONE, g1, 0.0))

    any_spec = pl.BlockSpec(memory_space=pl.ANY)
    return pl.pallas_call(
        body, name='scatter_rows',
        grid_spec=pltpu.PrefetchScalarGridSpec(
            num_scalar_prefetch=ONE, grid=(nw,),
            in_specs=[pl.BlockSpec((2, WIN), lambda w, t: (ZERO, w))] + [any_spec] * 2,
            out_specs=[pl.BlockSpec((WIN, dim), lambda w, t: (w, ZERO)), pl.BlockSpec((WIN, LANES), lambda w, t: (w, ZERO))],
            scratch_shapes=[pltpu.VMEM((2, FLAT, dim), BF16), pltpu.VMEM((2, FLAT, LANES), BF16), pltpu.VMEM((WIN, dim), F32),
                            pltpu.VMEM((2, WIN, LANES), F32), pltpu.SemaphoreType.DMA((4,))]),
        out_shape=[jax.ShapeDtypeStruct((tok, dim), BF16), jax.ShapeDtypeStruct((tok, LANES), F32)],
        compiler_params=params(ONE),
        cost_estimate=pl.CostEstimate(flops=8 * tok * 256 * dim, bytes_accessed=4 * tok * dim, transcendentals=ZERO),
    )(vec, pos, dx_rows, g_rows)


def combine_rows(vec, pos, tok_w, keep, r_main, r_over, own, tab):
    dim = keep.shape[ONE]
    nw = tab.nw
    per = nw // 4
    main_rows = r_main.shape[ZERO]

    def window(i, t):
        px = t[tab.x] if own else ONE - t[tab.x]
        return t[tab.seg] * (nw // 2) + px * per + i

    def body(tab_ref, pos_ref, w_ref, keep_ref, main_ref, over_ref, out_ref, kb, rb, acc, sem):
        i = pl.program_id(ZERO)
        slot = lax.rem(i, 2)
        seg = tab_ref[tab.seg]

        def fetch(step, to):
            win = window(step, tab_ref)
            for e in range(4):
                at = e * nw + win
                shift = jnp.where(seg == ONE, tab_ref[tab.list1 + e] - tab_ref[tab.mid + e], tab_ref[tab.list0 + e])

                def one(k, c):
                    row = tab_ref[tab.first + at] + shift + GR * k
                    put = pl.ds(mult(tab_ref[tab.flat + at] + GR * k, GR), GR)
                    pltpu.make_async_copy(keep_ref.at[pl.ds(mult(row, GR), GR)], kb.at[to, put], sem.at[to]).start()

                    @pl.when(row < main_rows)
                    def _():
                        pltpu.make_async_copy(main_ref.at[pl.ds(mult(row, GR), GR)], rb.at[to, put], sem.at[2 + to]).start()

                    @pl.when(row >= main_rows)
                    def _():
                        pltpu.make_async_copy(over_ref.at[pl.ds(mult(row - main_rows, GR), GR)], rb.at[to, put], sem.at[2 + to]).start()

                    return c

                lax.fori_loop(ZERO, tab_ref[tab.count + at], one, ZERO)

        @pl.when(i == ZERO)
        def _():
            kb[...] = jnp.zeros_like(kb)
            rb[...] = jnp.zeros_like(rb)
            fetch(ZERO, ZERO)

        @pl.when(i + ONE < per)
        def _():
            fetch(i + ONE, ONE - slot)

        w = window(i, tab_ref)

        def one_wait(k, c):
            pltpu.make_async_copy(keep_ref.at[pl.ds(ZERO, GR)], kb.at[slot, pl.ds(ZERO, GR)], sem.at[slot]).wait()
            pltpu.make_async_copy(main_ref.at[pl.ds(ZERO, GR)], rb.at[slot, pl.ds(ZERO, GR)], sem.at[2 + slot]).wait()
            return c

        lax.fori_loop(ZERO, sum(tab_ref[tab.count + e * nw + w] for e in range(4)), one_wait, ZERO)

        acc[...] = jnp.zeros_like(acc)

        def block(b, c):
            j = lax.broadcasted_iota(I32, (BLK, WIN), ZERO) + b * BLK
            rows = pl.ds(mult(b * BLK, BLK), BLK)
            y = (kb[slot, rows, :].astype(F32) + rb[slot, rows, :].astype(F32)).astype(BF16)
            acc[ZERO] += dot_tn(jnp.where(pos_ref[ZERO:ONE, :] == j, 1.0, 0.0).astype(BF16), y)
            acc[ONE] += dot_tn(jnp.where(pos_ref[ONE:2, :] == j, 1.0, 0.0).astype(BF16), y)
            return c

        lax.fori_loop(ZERO, flat_blocks(tab_ref, tab, w), block, ZERO)
        w0, w1, both = w_ref[:, ZERO:ONE], w_ref[:, ONE:2], w_ref[:, 2:3]
        out_ref[...] = jnp.where(both > 0.5, w0 * acc[ZERO] + w1 * acc[ONE], acc[ZERO] + acc[ONE]).astype(BF16)

    any_spec = pl.BlockSpec(memory_space=pl.ANY)
    return pl.pallas_call(
        body, name='combine_rows',
        grid_spec=pltpu.PrefetchScalarGridSpec(
            num_scalar_prefetch=ONE, grid=(per,),
            in_specs=[pl.BlockSpec((2, WIN), lambda i, t: (ZERO, window(i, t))),
                      pl.BlockSpec((WIN, 8), lambda i, t: (window(i, t), ZERO)), any_spec, any_spec, any_spec],
            out_specs=pl.BlockSpec((WIN, dim), lambda i, t: (i, ZERO)),
            scratch_shapes=[pltpu.VMEM((2, FLAT, dim), BF16), pltpu.VMEM((2, FLAT, dim), BF16), pltpu.VMEM((2, WIN, dim), F32),
                            pltpu.SemaphoreType.DMA((4,))]),
        out_shape=jax.ShapeDtypeStruct((per * WIN, dim), BF16),
        compiler_params=params(ONE),
        cost_estimate=pl.CostEstimate(flops=4 * per * WIN * 512 * dim, bytes_accessed=6 * per * WIN * dim, transcendentals=ZERO),
    )(vec, pos, tok_w, keep, r_main, r_over)


def solution(mesh):
    tp_n, ep_n = mesh.shape['tp'], mesh.shape['ep']
    fine = Mesh(mesh.devices.reshape(tp_n, ep_n // 2, 2), ('tp', 'x', 'c'))
    group = ('tp', 'x')
    every = ('tp', 'x', 'c')
    swap = [(ZERO, ONE), (ONE, ZERO)]

    def device_fn(x_loc, idx_loc, slot_loc, w_router, b_router, w_gu, b_gu, w_dn, b_dn, dy_loc):
        n_tok, dim = x_loc.shape
        n_experts = w_router.shape[ONE]
        n_loc, _, width = w_gu.shape
        units = width // 2
        nf = pl.cdiv(units, FT)
        tok = 4 * n_tok
        cap = 4 * (2 * n_tok * 2 // n_experts)
        tab = Table(tok // WIN)
        main_rows = cap
        tp_pos, x_pos, c_pos = lax.axis_index('tp'), lax.axis_index('x'), lax.axis_index('c')

        logits = jnp.dot(x_loc, w_router, preferred_element_type=F32) + b_router[None, :]
        hot = idx_loc[:, :, None] == jnp.arange(n_experts)[None, None, :]
        picked = jnp.sum(jnp.where(hot, logits[:, None, :], 0.0), axis=2)
        gate_w = jax.nn.softmax(picked, axis=ONE)
        mine = jnp.concatenate([idx_loc.astype(F32), slot_loc.astype(F32), gate_w, jnp.zeros((n_tok, 2), F32)], axis=ONE)
        wide = lax.all_gather(mine.T, every, axis=ZERO).reshape(tp_n, 2, 2, 8, n_tok)
        counts = jnp.where(wide[..., 2:4, :] >= ZERO, wide[..., ZERO:2, :], -1.0)
        counts = jnp.sum(counts[..., None] == jnp.arange(n_experts, dtype=F32), axis=(3, 4))
        counts = jnp.sum(counts, axis=ONE).reshape(tp_n, 2, 2, n_experts // 2)
        spill = jnp.max(jnp.sum((counts + GR - ONE) // GR * GR, axis=3)) > cap
        shared = lax.dynamic_index_in_dim(wide, c_pos, 2, keepdims=False)
        shared = shared.transpose(2, ZERO, ONE, 3).reshape(8, tok)
        x_all = lax.all_gather(x_loc, group, axis=ZERO, tiled=True)
        d_all = lax.all_gather(dy_loc, group, axis=ZERO, tiled=True)
        idx_t, slot_t, w_t = shared[ZERO:2].astype(I32), shared[2:4].astype(I32), shared[4:6]
        vec, pos = make_table(idx_t, slot_t, x_pos, c_pos, tp_pos, tab)
        both_t = ((pos[ZERO] >= ZERO) & (pos[ONE] >= ZERO)).astype(F32)
        tok_w = jnp.concatenate([w_t, both_t[None], jnp.zeros((5, tok), F32)], axis=ZERO).T

        wg = (split_weights(w_gu),)
        wd = (jnp.pad(w_dn, ((ZERO, ZERO), (ZERO, nf * FT - units), (ZERO, ZERO))),)
        bg = jnp.pad(b_gu.reshape(n_loc, units, 2), ((ZERO, ZERO), (ZERO, nf * FT - units), (ZERO, ZERO)))
        bg = bg.reshape(n_loc, nf, FT, 2).transpose(ZERO, ONE, 3, 2).reshape(n_loc, nf, ONE, 2 * FT)
        bd = jnp.where(tp_pos == ZERO, b_dn, 0.0).reshape(n_loc, ONE, dim)
        trade = functools.partial(lax.ppermute, axis_name='c', perm=swap)
        wg += (trade(wg[ZERO]),)
        wd += (trade(wd[ZERO]),)
        bg = jnp.concatenate([bg, trade(bg)], axis=ZERO)
        bd = jnp.concatenate([bd, trade(bd)], axis=ZERO)

        x_rows = gather_rows(vec, pos, x_all, cap, tab)
        x_back = trade(x_rows[ONE])
        vec_oth = trade(vec)
        h_all, a_own, a_oth, keep, s_main, s_over = expert_forward(vec, x_rows, wg, wd, bg, bd, main_rows, tab)
        other_tp = functools.partial(lax.ppermute, axis_name='tp', perm=swap)
        r_main = other_tp(s_main)
        r_over = lax.cond(spill, other_tp, lambda b: b, s_over)
        a_back = trade(a_oth)

        d_rows = gather_rows(vec, pos, d_all, cap, tab, w_t)
        d_back = trade(d_rows[ONE])
        dh_own, dh_oth, dx_rows, g_rows, sbg, sbd = expert_backward(vec, d_rows, wg, wd, bd, h_all, tab)
        dh_back = trade(dh_oth)
        dx_tok, g_tok = scatter_rows(vec, pos, dx_rows, g_rows, tok, tab)
        g_sum = lax.psum_scatter(g_tok, group, scatter_dimension=ZERO, tiled=True)[:, :2]
        dx_sum = lax.psum_scatter(dx_tok, group, scatter_dimension=ZERO, tiled=True)
        grad_w_gu, grad_w_dn = weight_grads((vec, vec_oth), (x_rows[ZERO], x_back), (d_rows[ZERO], d_back), (dh_own, dh_back), (a_own, a_back), tab, width)

        y_out = combine_rows(vec, pos, tok_w, keep, r_main, r_over, False, tab)
        y_in = lax.ppermute(y_out, 'x', swap)
        y_own = combine_rows(vec, pos, tok_w, keep, r_main, r_over, True, tab)
        kept = slot_loc >= ZERO
        here = idx_loc // 4 == x_pos
        y_k = jnp.where(here[:, :, None], y_own.astype(F32)[:, None, :], y_in.astype(F32)[:, None, :])
        y_sum = jnp.sum(jnp.where(kept[:, :, None], gate_w[:, :, None] * y_k, 0.0), axis=ONE).astype(BF16)
        all_here = jnp.all(kept & here, axis=ONE, keepdims=True)
        all_there = jnp.all(kept & ~here, axis=ONE, keepdims=True)
        moe_out = jnp.where(all_here, y_own, jnp.where(all_there, y_in, y_sum))

        d_picked = g_sum - gate_w * jnp.sum(g_sum, axis=ONE, keepdims=True)
        d_logits = jnp.sum(jnp.where(hot, d_picked[:, :, None], 0.0), axis=ONE)
        d_logits_b = d_logits.astype(BF16)
        router = jnp.einsum('td,te->de', x_loc, d_logits_b, preferred_element_type=F32)
        router = jnp.concatenate([router, jnp.sum(d_logits, axis=ZERO, keepdims=True)], axis=ZERO)
        router = lax.psum(router, every)
        grad_w_router, grad_b_router = router[:dim], router[dim]
        grad_x = (dx_sum.astype(F32) + jnp.einsum('te,de->td', d_logits_b, w_router, preferred_element_type=F32)).astype(BF16)

        sbg = sbg[:n_loc] + trade(sbg[n_loc:])
        grad_b_gu = sbg.reshape(n_loc, nf, 2, FT).transpose(ZERO, ONE, 3, 2).reshape(n_loc, nf * FT * 2)[:, :width]
        grad_b_dn = (sbd[:n_loc] + trade(sbd[n_loc:])).reshape(n_loc, dim)
        return (moe_out, grad_x, grad_w_gu, grad_b_gu, grad_w_dn, grad_b_dn, grad_w_router, grad_b_router)

    ep = ('x', 'c')
    toks = P(('x', 'c', 'tp'), None)
    in_specs = (toks, toks, toks, P(None, None), P(None), P(ep, None, 'tp'), P(ep, 'tp'), P(ep, 'tp', None), P(ep, None), toks)
    out_specs = (toks, toks, P(ep, None, 'tp'), P(ep, 'tp'), P(ep, 'tp', None), P(ep, None), P(None, None), P(None))

    return jax.shard_map(device_fn, mesh=fine, in_specs=in_specs, out_specs=out_specs, check_vma=False)
```

time: 2060 us -> 1920 us (0.932)
  the two profiles are of different devices: /device:TPU:7 before, /device:TPU:3 now
where the time goes in v2:
time: 1920 us; the launch traced here: 1910 us
  Pallas kernels  1070 us (56%)
  waiting for transfers between devices  628 us (33%)
  blocking collectives  92.7 us (5%)
  local copies, waits for them, and re-layouts  42.7 us (2%)
  other arithmetic  32.8 us (2%)
    pallas_call x1, Pallas kernels, weight_grads(): pl.pallas_call(body, name='weight_grads', grid_spec=pltpu.PrefetchScalarG...  372 us
    ppermute x1, waiting for transfers between devices, device_fn(): r_main = other_tp(s_main)  306 us
    pallas_call x1, Pallas kernels, expert_backward(): pl.pallas_call(body, name='expert_backward', grid_spec=pltpu.PrefetchScal...  299 us
    pallas_call x1, Pallas kernels, expert_forward(): pl.pallas_call(body, name='expert_forward', grid_spec=pltpu.PrefetchScala...  232 us
    all_gather x1, waiting for transfers between devices, device_fn(): d_all = lax.all_gather(dy_loc, group, axis=ZERO, tiled=True)  129 us
    all_gather x1, blocking collectives, device_fn(): lax.all_gather(mine.T, every, axis=ZERO).reshape(tp_n, 2, 2, 8, n_tok)  92.7 us
    ppermute x1, waiting for transfers between devices, device_fn(): grad_b_dn = (sbd[:n_loc] + trade(sbd[n_loc:])).reshape(n_loc, dim)  91.1 us
    ppermute x1, waiting for transfers between devices, device_fn(): y_in = lax.ppermute(y_out, 'x', swap)  72.5 us
  transfers between devices with their start and end apart: 18, of which 5 were waited for; matrix products, arithmetic and copies ran while one was open for 5% of the time, Pallas kernels for 9%

profile of v2, /device:TPU:3, one launch (start us, length us, event | category | flops | bytes accessed | tf_op | source)
XLA Modules:
  0.0 1908.1 jit_solution(16542692694675389020)
XLA Ops:
  7.2 0.7 all-gather.4.cloned.1.call-update
  8.0 57.4 %split_weights.1.go = bf16[2,6,2304,1024]{3,2,1,0:T(8,128)(2,1)} custom-call(bf16[2,2304,5760]{2,1,0:T(8,128)(2,1)} %w_ref.1), custom_call_target="tpu_custom_call" | custom-call | flops 13589544960 | bytes 106168320 | tf_op jit(solution)/shard_map/split_weights/pallas_call | solution.py:143
  65.3 0.7 collective-permute-start.1
  66.1 20.1 %pad.8.do = bf16[2,3072,2304]{2,1,0:T(8,128)(2,1)} pad(bf16[2,2880,2304]{2,1,0:T(8,128)(2,1)} %param.19, bf16[]{:T(256)} %constant.238.clone.1), padding=0_0x0_192x0_0 | pad | bytes 54853632 | tf_op jit(solution)/shard_map/jit(_pad)/pad | solution.py:970
  86.2 4.7 reshape.310
  90.9 2.0 pad.9
  92.9 1.2 copy.163
  94.2 0.5 collective-permute-start.3
  94.8 3.6 convolution_add_fusion
  98.6 0.2 copy.141
  98.8 0.8 copy-done.1
  99.6 0.2 broadcast_divide_fusion
  99.8 0.2 copy.143
  100.2 92.7 %all-gather = f32[64,1024]{1,0:T(8,128)S(1)} all-gather(f32[8,1024]{1,0:T(8,128)S(1)} %maximum_bitcast_fusion), channel_id=2, replica_groups=mesh['tp'=2,'x'=2,'c'=2] {'tp','x','c'}, dimensions={0}, use_global_device_ids=true | all-gather | bytes 294912 | tf_op jit(solution)/shard_map/all_gather | solution.py:955
  193.0 0.6 fusion.41
  193.7 0.3 and_select_fusion.3
  194.2 0.2 fusion.36
  195.0 0.2 fusion
  195.6 0.3 copy.146
  197.5 0.8 select_reduce_fusion.1.refs_0_.pos_ref
  198.6 0.7 concatenate.19.tab_ref.tab0
  199.3 0.7 pad_maximum_fusion.bg_ref
  200.0 24.7 %gather_rows.2 = (bf16[2,2048,2304]{2,1,0:T(8,128)(2,1)}, bf16[2,2048,2304]{2,1,0:T(8,128)(2,1)}) custom-call(s32[342]{0:T(512)} %concatenate.19.tab_ref.tab0, s32[2,4096]{1,0:T(2,128)} %select_reduce_fusion.1.refs_0_.pos_ref, bf16[4096,2304]{1,0:T(8,128)(2,1)} %all-gather.4.cloned.1.call-done.refs_1_), custom_call_target="tpu_custom_call" | custom-call | flops 19327352832 | bytes 37748736 | tf_op jit(solution)/shard_map/gather_rows/pallas_call | solution.py:250
  224.7 128.5 %all-gather.6.cloned.1.call-done.refs_2_ = bf16[4096,2304]{1,0:T(8,128)(2,1)} async-done(((bf16[1024,2304]{1,0:T(8,128)(2,1)}), bf16[4096,2304]{1,0:T(8,128)(2,1)}) %all-gather.6.cloned.1.call-update) | async-done | bytes 18874384 | tf_op jit(solution)/shard_map/all_gather | solution.py:963
  353.2 25.0 %gather_rows.3 = (bf16[2,2048,2304]{2,1,0:T(8,128)(2,1)}, bf16[2,2048,2304]{2,1,0:T(8,128)(2,1)}) custom-call(s32[342]{0:T(512)} %concatenate.19.tab_ref.tab0, s32[2,4096]{1,0:T(2,128)} %select_reduce_fusion.1.refs_0_.pos_ref, f32[2,4096]{1,0:T(2,128)} %bitcast.76, bf16[4096,2304]{1,0:T(8,128)(2,1)} %all-gather.6.cloned.1.call-done.refs_2_), custom_call_target="tpu_custom_call" | custom-call | flops 19327352832 | bytes 37748736 | tf_op jit(solution)/shard_map/gather_rows/pallas_call | solution.py:250
  378.2 232.0 %expert_forward.1 = (f32[4,2048,6144]{2,1,0:T(8,128)}, bf16[2,2048,3072]{2,1,0:T(8,128)(2,1)}, bf16[2,2048,3072]{2,1,0:T(8,128)(2,1)}, bf16[4160,2304]{1,0:T(8,1...) custom-call(s32[342]{0:T(512)} %concatenate.19.tab_ref.tab0, ...), custom_call_target="tpu_custom_call" | custom-call | flops 173946175488 | bytes 169869312 | tf_op jit(solution)/shard_map/expert_forward/pallas_call | solution.py:465
  610.2 299.2 %expert_backward.1 = (bf16[2,2048,6144]{2,1,0:T(8,128)(2,1)}, bf16[2,2048,6144]{2,1,0:T(8,128)(2,1)}, bf16[4,2048,2304]{2,1,0:T(8,128)(2,1)}, bf16[4,2048,128]{2...) custom-call(s32[342]{0:T(512)} %concatenate.19.tab_ref.tab0, ...), custom_call_target="tpu_custom_call" | custom-call | flops 173946175488 | bytes 169869312 | tf_op jit(solution)/shard_map/expert_backward/pallas_call | solution.py:617
  909.5 6.4 collective-permute-start.10
  915.9 31.9 %scatter_rows.1 = (bf16[4096,2304]{1,0:T(8,128)(2,1)}, f32[4096,128]{1,0:T(8,128)}) custom-call(s32[342]{0:T(512)} %concatenate.19.tab_ref.tab0, s32[2,4096]{1,0:T(2,128)} %select_reduce_fusion.1.refs_0_.pos_ref, bf16[4,2048,2304]{2,1,0:T(8,128)(2,1)} %get-tuple-element.41.x_ref, bf16[4,2048,128]{2,1,0:T(8,128)(2,1)} %get-tuple-element.42.g_ref), custom_call_target="tpu_custom_call" | custom-call | flops 19327352832 | bytes 37748736 | tf_op jit(solution)/shard_map/scatter_rows/pallas_call | solution.py:830
  947.9 29.0 %reduce-scatter.5.cloned.1.call-done = f32[1024,128]{1,0:T(8,128)} async-done(((f32[4096,128]{1,0:T(8,128)}), f32[1024,128]{1,0:T(8,128)}) %reduce-scatter.5.cloned.1.call-update) | async-done | bytes 524304 | tf_op jit(solution)/shard_map/reduce_scatter | solution.py:994
  976.9 1.2 slice_reduce_fusion
  978.2 1.4 multiply_subtract_fusion
  979.6 0.2 copy.165
  980.0 3.1 convolution_bitcast_fusion
  983.0 0.6 pad_maximum_fusion.1
  983.8 0.5 reduce-scatter.3.cloned.1.call-update
  984.3 0.9 collective-permute-start.11
  985.2 0.2 convert_reduce_fusion
  985.4 0.4 collective-permute-start.8
  986.2 0.6 reduce_max.29
  987.5 0.4 collective-permute-start.13
  988.0 91.1 %collective-permute-done.13 = f32[2,1,2304]{2,1,0:T(1,128)S(1)} collective-permute-done((f32[2,1,2304]{2,1,0:T(1,128)S(1)}, f32[2,1,2304]{2,1,0:T(1,128)S(1)}, u32[]{:S(2)}, u32[]{:S(2)}) %collective-permute-start.13) | collective-permute-done | bytes 18464 | tf_op jit(solution)/shard_map/ppermute | solution.py:1020
  1079.0 0.2 collective-permute-start.5
  1079.5 2.0 copy.161
  1081.5 305.6 %collective-permute-done.5.main_ref = bf16[2048,2304]{1,0:T(8,128)(2,1)} collective-permute-done((bf16[2048,2304]{1,0:T(8,128)(2,1)}, bf16[2048,2304]{1,0:T(8,128)(2,1)}, u32[]{:S(2)}, u32[]{:S(2)}) %collective-permute-start.5) | collective-permute-done | bytes 9437216 | tf_op jit(solution)/shard_map/ppermute | solution.py:985
  1387.1 0.6 collective-permute-start.12
  1387.7 15.7 combine_rows.3
  1403.6 0.6 copy.186
  1404.4 1.1 copy.166
  1405.5 2.2 reshape.315
  1407.6 0.6 slice.100
  1408.3 5.0 fusion.42
  1413.3 1.5 slice.101
  1414.8 1.3 slice_reduce_fusion.1
  1416.1 15.5 combine_rows.2
  1431.6 3.0 convert_element_type.110
  1434.6 72.5 %collective-permute-done.6 = bf16[1024,2304]{1,0:T(8,128)(2,1)} collective-permute-done((bf16[1024,2304]{1,0:T(8,128)(2,1)}, bf16[1024,2304]{1,0:T(8,128)(2,1)}, u32[]{:S(2)}, u32[]{:S(2)}) %collective-permute-start.6) | collective-permute-done | bytes 4718624 | tf_op jit(solution)/shard_map/ppermute | solution.py:999
  1507.1 0.9 collective-permute-start.7
  1508.0 3.2 convert_element_type.111
  1511.2 5.0 select_reduce_fusion
  1516.3 4.7 select_select_fusion
  1520.9 8.2 add_convert_fusion
  1529.2 0.5 copy-done.22
  1529.7 371.6 %weight_grads.1 = (bf16[2,2304,5760]{2,1,0:T(8,128)(2,1)}, bf16[2,2880,2304]{2,1,0:T(8,128)(2,1)}) custom-call(s32[342]{0:T(512)} %concatenate.19.tab_ref.tab0, s32[342]{0:T(512)} %copy-done.22, bf16[2,2048,2304]{2,1,0:T(8,128)(2,1)} %get-tuple-element.33.xo.x0, bf16[2,2048,2304]{2,1,0:T(8,128)(2,1)} %collective-permute-done.8.x1, ...), custom_call_target="tpu_custom_call" | custom-call | flops 173946175488 | bytes 84934656 | tf_op jit(solution)/shard_map/weight_grads/pallas_call | solution.py:755
  (148 shorter events, 5.1 us)
Async XLA Ops:
  7.2 87.7 %copy-start = (bf16[2304,8]{0,1:T(8,128)(2,1)S(1)}, bf16[2304,8]{0,1:T(8,128)(2,1)}, u32[]{:S(2)}) copy-start(bf16[2304,8]{0,1:T(8,128)(2,1)} %param.15) | copy-start | bytes 110596
  7.2 192.8 %all-gather.4.cloned.1.call-start = ((), (), s32[]{:S(2)}) async-start(), calls=%async_computation.2 | async-start | bytes 23592960 | tf_op jit(solution)/shard_map/all_gather | solution.py:962
  7.9 345.3 %all-gather.6.cloned.1.call-start = ((), (), s32[]{:S(2)}) async-start(), calls=%async_computation.3 | async-start | bytes 23592960 | tf_op jit(solution)/shard_map/all_gather | solution.py:963
  65.3 312.9 %collective-permute-start.1 = (bf16[2,6,2304,1024]{3,2,1,0:T(8,128)(2,1)}, bf16[2,6,2304,1024]{3,2,1,0:T(8,128)(2,1)}, u32[]{:S(2)}, u32[]{:S(2)}) collective-permute-start(bf16[2,6,2304,1024]{3,2,1,0:T(8,128)(2,1)} %split_weights.1.go), channel_id=1, source_target_pairs={{0,1},{1,0},{2,3},{3,2},{4,5},{5,4},{6,7},{7,6}} | collective-permute-start | bytes 169869312 | tf_op jit(solution)/shard_map/ppermute | solution.py:975
  66.0 20.2 %copy-start.12 = (f32[2,5760]{1,0:T(2,128)S(1)}, f32[2,5760]{1,0:T(2,128)}, u32[]{:S(2)}) copy-start(f32[2,5760]{1,0:T(2,128)} %param.18) | copy-start | bytes 138244
  66.0 910.9 %reduce-scatter.5.cloned.1.call-start = ((), (), s32[]{:S(2)}) async-start(), calls=%async_computation.5 | async-start | bytes 2621440 | tf_op jit(solution)/shard_map/reduce_scatter | solution.py:994
  86.2 8.6 copy-start.19
  86.2 8.7 copy-start.6
  86.2 8.7 copy-start.21
  86.2 292.0 %collective-permute-start.2 = (bf16[2,3072,2304]{2,1,0:T(8,128)(2,1)}, bf16[2,3072,2304]{2,1,0:T(8,128)(2,1)}, u32[]{:S(2)}, u32[]{:S(2)}) collective-permute-start(bf16[2,3072,2304]{2,1,0:T(8,128)(2,1)} %pad.8.do), channel_id=1, source_target_pairs={{0,1},{1,0},{2,3},{3,2},{4,5},{5,4},{6,7},{7,6}} | collective-permute-start | bytes 84934664 | tf_op jit(solution)/shard_map/ppermute | solution.py:976
  90.9 9.2 copy-start.16
  94.2 105.1 %collective-permute-start.3 = (f32[2,6,1,1024]{3,2,1,0:T(1,128)S(1)}, f32[2,6,1,1024]{3,2,1,0:T(1,128)S(1)}, u32[]{:S(2)}, u32[]{:S(2)}) collective-permute-start(f32[2,6,1,1024]{3,2,1,0:T(1,128)S(1)} %reshape.312), channel_id=1, source_target_pairs={{0,1},{1,0},{2,3},{3,2},{4,5},{5,4},{6,7},{7,6}} | collective-permute-start | bytes 147464 | tf_op jit(solution)/shard_map/ppermute | solution.py:977
  94.8 104.5 %collective-permute-start.4 = (f32[2,1,2304]{2,1,0:T(1,128)S(1)}, f32[2,1,2304]{2,1,0:T(1,128)S(1)}, u32[]{:S(2)}, u32[]{:S(2)}) collective-permute-start(f32[2,1,2304]{2,1,0:T(1,128)S(1)} %reshape.313), channel_id=1, source_target_pairs={{0,1},{1,0},{2,3},{3,2},{4,5},{5,4},{6,7},{7,6}} | collective-permute-start | bytes 55304 | tf_op jit(solution)/shard_map/ppermute | solution.py:978
  98.6 101.4 %copy-start.13 = (f32[1024]{0:T(1024)}, f32[1024]{0:T(1024)S(1)}, u32[]{:S(2)}) copy-start(f32[1024]{0:T(1024)S(1)} %get-tuple-element.68) | copy-start | bytes 12292
  98.8 0.8 copy-start.1
  100.0 94.0 %copy-start.10 = (f32[1024,2]{0,1:T(2,128)}, f32[1024,2]{0,1:T(2,128)S(1)}, u32[]{:S(2)}) copy-start(f32[1024,2]{0,1:T(2,128)S(1)} %copy.143) | copy-start | bytes 24580
  193.0 1.1 copy-start.3
  199.3 25.4 %copy-start.20 = (f32[4,1,2304]{2,1,0:T(1,128)}, f32[4,1,2304]{2,1,0:T(1,128)S(1)}, u32[]{:S(2)}) copy-start(f32[4,1,2304]{2,1,0:T(1,128)S(1)} %constant_dynamic-update-slice_fusion.bd_ref) | copy-start | bytes 110596
  909.5 619.7 %collective-permute-start.10 = (bf16[2,2048,6144]{2,1,0:T(8,128)(2,1)}, bf16[2,2048,6144]{2,1,0:T(8,128)(2,1)}, u32[]{:S(2)}, u32[]{:S(2)}) collective-permute-start(bf16[2,2048,6144]{2,1,0:T(8,128)(2,1)} %get-tuple-element.46), channel_id=1, source_target_pairs={{0,1},{1,0},{2,3},{3,2},{4,5},{5,4},{6,7},{7,6}} | collective-permute-start | bytes 150994944 | tf_op jit(solution)/shard_map/ppermute | solution.py:992
  915.9 62.3 %copy-start.2 = (f32[1024,2]{1,0:T(8,128)S(1)}, f32[1024,2]{1,0:T(8,128)}, u32[]{:S(2)}) copy-start(f32[1024,2]{1,0:T(8,128)} %copy-done.1) | copy-start | bytes 24580
  915.9 62.3 %copy-start.14 = (f32[1024]{0:T(1024)S(1)}, f32[1024]{0:T(1024)}, u32[]{:S(2)}) copy-start(f32[1024]{0:T(1024)} %copy-done.13) | copy-start | bytes 12292
  915.9 63.9 %copy-start.7 = (s32[1024,2]{0,1:T(2,128)S(1)}, s32[1024,2]{0,1:T(2,128)}, u32[]{:S(2)}) copy-start(s32[1024,2]{0,1:T(2,128)} %param.13) | copy-start | bytes 24580
  947.8 465.5 %all-reduce.4.cloned.1.call-start = ((), (), s32[]{:S(2)}) async-start(), calls=%async_computation.6 | async-start | bytes 155648 | tf_op jit(solution)/shard_map/psum | solution.py:1014
  983.7 537.2 %reduce-scatter.3.cloned.1.call-start = ((), (), s32[]{:S(2)}) async-start(), calls=%async_computation.4 | async-start | bytes 23592960 | tf_op jit(solution)/shard_map/reduce_scatter | solution.py:995
  983.7 1.4 copy-start.4
  983.8 3.7 copy-start.15
  984.3 544.9 %collective-permute-start.11 = (bf16[2,2048,3072]{2,1,0:T(8,128)(2,1)}, bf16[2,2048,3072]{2,1,0:T(8,128)(2,1)}, u32[]{:S(2)}, u32[]{:S(2)}) collective-permute-start(bf16[2,2048,3072]{2,1,0:T(8,128)(2,1)} %get-tuple-element.48), channel_id=1, source_target_pairs={{0,1},{1,0},{2,3},{3,2},{4,5},{5,4},{6,7},{7,6}} | collective-permute-start | bytes 75497480 | tf_op jit(solution)/shard_map/ppermute | solution.py:987
  985.4 543.7 %collective-permute-start.8 = (bf16[2,2048,2304]{2,1,0:T(8,128)(2,1)}, bf16[2,2048,2304]{2,1,0:T(8,128)(2,1)}, u32[]{:S(2)}, u32[]{:S(2)}) collective-permute-start(bf16[2,2048,2304]{2,1,0:T(8,128)(2,1)} %get-tuple-element.34.xt), channel_id=1, source_target_pairs={{0,1},{1,0},{2,3},{3,2},{4,5},{5,4},{6,7},{7,6}} | collective-permute-start | bytes 56623112 | tf_op jit(solution)/shard_map/ppermute | solution.py:981
  985.8 543.3 %collective-permute-start.9 = (bf16[2,2048,2304]{2,1,0:T(8,128)(2,1)}, bf16[2,2048,2304]{2,1,0:T(8,128)(2,1)}, u32[]{:S(2)}, u32[]{:S(2)}) collective-permute-start(bf16[2,2048,2304]{2,1,0:T(8,128)(2,1)} %get-tuple-element.39.dt_in), channel_id=1, source_target_pairs={{0,1},{1,0},{2,3},{3,2},{4,5},{5,4},{6,7},{7,6}} | collective-permute-start | bytes 56623112 | tf_op jit(solution)/shard_map/ppermute | solution.py:990
  987.5 91.9 %copy-start.5 = (s32[2,4096]{1,0:T(2,128)S(1)}, s32[2,4096]{1,0:T(2,128)}, u32[]{:S(2)}) copy-start(s32[2,4096]{1,0:T(2,128)} %select_reduce_fusion.1.refs_0_.pos_ref) | copy-start | bytes 98308
  987.5 91.9 %copy-start.8 = (f32[2,2,2,1024]{3,0,2,1:T(2,128)S(1)}, f32[2,2,2,1024]{3,0,2,1:T(2,128)}, u32[]{:S(2)}) copy-start(f32[2,2,2,1024]{3,0,2,1:T(2,128)} %get-tuple-element.70) | copy-start | bytes 98308
  987.5 93.9 %copy-start.9 = (f32[4,6,1,1024]{3,2,1,0:T(1,128)S(1)}, f32[4,6,1,1024]{3,2,1,0:T(1,128)}, u32[]{:S(2)}) copy-start(f32[4,6,1,1024]{3,2,1,0:T(1,128)} %get-tuple-element.50) | copy-start | bytes 294916
  987.5 91.5 %collective-permute-start.13 = (f32[2,1,2304]{2,1,0:T(1,128)S(1)}, f32[2,1,2304]{2,1,0:T(1,128)S(1)}, u32[]{:S(2)}, u32[]{:S(2)}) collective-permute-start(f32[2,1,2304]{2,1,0:T(1,128)S(1)} %slice.87), channel_id=1, source_target_pairs={{0,1},{1,0},{2,3},{3,2},{4,5},{5,4},{6,7},{7,6}} | collective-permute-start | bytes 55304 | tf_op jit(solution)/shard_map/ppermute | solution.py:1020
  1079.0 308.1 %collective-permute-start.5 = (bf16[2048,2304]{1,0:T(8,128)(2,1)}, bf16[2048,2304]{1,0:T(8,128)(2,1)}, u32[]{:S(2)}, u32[]{:S(2)}) collective-permute-start(bf16[2048,2304]{1,0:T(8,128)(2,1)} %get-tuple-element.36), channel_id=1, source_target_pairs={{0,4},{4,0},{1,5},{5,1},{2,6},{6,2},{3,7},{7,3}} | collective-permute-start | bytes 28311560 | tf_op jit(solution)/shard_map/ppermute | solution.py:985
  1387.1 16.4 collective-permute-start.12
  1387.7 15.8 copy-start.17
  1403.5 103.7 %collective-permute-start.6 = (bf16[1024,2304]{1,0:T(8,128)(2,1)}, bf16[1024,2304]{1,0:T(8,128)(2,1)}, u32[]{:S(2)}, u32[]{:S(2)}) collective-permute-start(bf16[1024,2304]{1,0:T(8,128)(2,1)} %combine_rows.3), channel_id=1, source_target_pairs={{0,2},{2,0},{1,3},{3,1},{4,6},{6,4},{5,7},{7,5}} | collective-permute-start | bytes 14155784 | tf_op jit(solution)/shard_map/ppermute | solution.py:999
  1431.6 75.6 %copy-start.18 = (s32[342]{0:T(512)S(1)}, s32[342]{0:T(512)}, u32[]{:S(2)}) copy-start(s32[342]{0:T(512)} %concatenate.19.tab_ref.tab0) | copy-start | bytes 4108
  1434.6 76.6 %copy-start.11 = (f32[1024,2]{0,1:T(2,128)S(1)}, f32[1024,2]{0,1:T(2,128)}, u32[]{:S(2)}) copy-start(f32[1024,2]{0,1:T(2,128)} %copy-done.10) | copy-start | bytes 24580
  1507.1 22.0 %collective-permute-start.7 = (s32[342]{0:T(512)S(1)}, s32[342]{0:T(512)S(1)}, u32[]{:S(2)}, u32[]{:S(2)}) collective-permute-start(s32[342]{0:T(512)S(1)} %copy-done.18), channel_id=1, source_target_pairs={{0,1},{1,0},{2,3},{3,2},{4,5},{5,4},{6,7},{7,6}} | collective-permute-start | bytes 4112 | tf_op jit(solution)/shard_map/ppermute | solution.py:982
  1508.0 8.2 slice-start
  1511.2 5.0 slice-start.1
  1529.1 0.6 copy-start.22
Sparse Core Ops, SparseCore 0:
  9.8 171.2 all-gather.3
  182.9 170.2 all-gather.5
  947.9 28.9 reduce-scatter.4
  983.8 39.9 all-reduce.3
  1026.7 270.1 reduce-scatter.2
